TPU v7x, 32 devices: a whole 2x2x4 slice. The times are simulated.
32 devices in a mesh: col: 4 (over z), row: 8 (over y, x, core).
Axes of the slice: x: 2, y: 2, z: 4, core: 2. Of those that a mesh axis runs over, the one named last changes fastest.
Arguments:
- psi_init: float32 [2048, 2, 2048], P('row', None, 'col')
- left_env: float32 [2048, 14, 2048], P('row')
- mpo_tensor: float32 [14, 14, 2, 2], replicated
- right_env: float32 [2048, 14, 2048], P('col')
Outputs:
- output 1: float32 [4], replicated
- output 2: float32 [4], replicated
- output 3: float32 [2048, 2, 2048], P('row', None, 'col')
All inputs are finite; a program needn't handle non-finite values.
Results may differ from a plain program's by a relative error of at most 0.001.
Values sent between devices are 32-bit elements.
A program may use at most 1 GiB of HBM per device.

v0:
```python
import jax
import jax.numpy as jnp
from jax import lax
from jax.sharding import PartitionSpec as P

LANCZOS_STEPS = 4
EXACT_PREC = lax.Precision.HIGHEST


def solution(mesh):
    all_axes = ("row", "col")

    def global_dot(left_vec, right_vec):
        return lax.psum(jnp.sum(left_vec * right_vec), all_axes)

    def local_steps(psi_blk, left_blk, mpo_tensor, right_blk):
        left_cols = lax.all_to_all(left_blk, "row", 2, 0, tiled=True)

        def apply_ham(vec_blk):
            vec_rows = lax.all_gather(vec_blk, "row", axis=0, tiled=True)
            t_one = jnp.einsum("alc,asb->lcsb", left_cols, vec_rows, precision=EXACT_PREC, preferred_element_type=jnp.float32)
            t_two = jnp.einsum("lcsb,lrst->cbrt", t_one, mpo_tensor, precision=EXACT_PREC, preferred_element_type=jnp.float32)
            y_part = jnp.einsum("cbrt,brd->ctd", t_two, right_blk, precision=EXACT_PREC, preferred_element_type=jnp.float32)
            return lax.psum_scatter(y_part, "col", scatter_dimension=2, tiled=True)

        vec_cur = psi_blk / jnp.sqrt(global_dot(psi_blk, psi_blk))
        vec_prev = jnp.zeros_like(vec_cur)
        beta_prev = jnp.zeros((), jnp.float32)
        alpha_list = []
        beta_list = []
        for step_idx in range(LANCZOS_STEPS):
            work_vec = apply_ham(vec_cur)
            alpha_val = global_dot(vec_cur, work_vec)
            work_vec = work_vec - alpha_val * vec_cur - beta_prev * vec_prev
            beta_val = jnp.sqrt(global_dot(work_vec, work_vec))
            vec_prev = vec_cur
            vec_cur = work_vec / beta_val
            beta_prev = beta_val
            alpha_list.append(alpha_val)
            beta_list.append(beta_val)
        return jnp.stack(alpha_list), jnp.stack(beta_list), vec_cur

    return jax.shard_map(local_steps, mesh=mesh, in_specs=(P("row", None, "col"), P("row", None, None), P(), P("col", None, None)), out_specs=(P(), P(), P("row", None, "col")), check_vma=False)
```

profile of v0, /device:TPU:0, one launch (start us, length us, event | category | flops | bytes accessed | tf_op | source)
XLA Modules:
  0.0 2367.7 jit_solution(6096869170120661892)
XLA Ops:
  7.2 33.2 %copy.32 = f32[256,14,2048]{0,1,2:T(8,128)} copy(f32[256,14,2048]{2,0,1:T(8,128)} %param.5) | data formatting | bytes 58720256 | tf_op args[1]
  40.4 7.2 all-to-all-start
  47.6 1.7 multiply_reduce_fusion.8
  49.3 396.9 %psum.63 = f32[]{:T(128)} all-reduce(f32[]{:T(128)} %multiply_reduce_fusion.8), channel_id=1, replica_groups=mesh['col'=4,'row'=8] {'row','col'}, use_global_device_ids=true, to_apply=%region_1.0 | all-reduce | flops 1 | bytes 8 | tf_op jit(solution)/shard_map/psum | solution.py:14
  448.9 33.5 %copy.34 = f32[8,256,14,256]{3,1,0,2:T(8,128)} copy(f32[8,256,14,256]{1,2,3,0:T(8,128)} %bitcast.4) | data formatting | bytes 58720256 | tf_op jit(solution)/shard_map/all_to_all | solution.py:17
  482.5 21.1 all-gather.5.cloned.1.call-done
  503.5 103.3 %fusion.20 = f32[14,256,2,512,1]{1,3,0,2,4:T(8,128)} fusion(f32[2048,14,256,1]{2,0,1,3:T(8,128)} %bitcast.111, f32[2048,2,512]{0,2,1:T(8,128)} %all-gather.5.cloned.1.call-done), kind=kOutput, calls=%fused_computation.24 | convolution fusion | flops 90194313216 | bytes 52428800 | tf_op jit(solution)/shard_map/alc,asb->lcsb/dot_general | solution.py:21
  606.9 19.5 copy.53
  626.4 19.3 convolution_bitcast_fusion.3
  645.7 114.4 %fusion.32 = f32[256,2,2048]{0,2,1:T(8,128)} fusion(f32[512,14,2048]{2,0,1:T(8,128)} %param.7, f32[256,512,14,2]{1,2,3,0:T(8,128)} %convolution_bitcast_fusion.3), kind=kOutput, calls=%fused_computation.28 | convolution fusion | flops 90194313216 | bytes 77594624 | tf_op jit(solution)/shard_map/cbrt,brd->ctd/dot_general | solution.py:23
  760.2 76.8 %reduce-scatter.5.cloned.1.call-done = f32[256,2,512]{0,2,1:T(8,128)} async-done(((f32[256,2,2048]{0,2,1:T(8,128)}), f32[256,2,512]{0,2,1:T(8,128)}) %reduce-scatter.5.cloned.1.call-update) | async-done | bytes 1048592 | tf_op jit(solution)/shard_map/reduce_scatter | solution.py:24
  837.0 2.1 multiply_reduce_fusion.7
  839.1 40.5 %psum.64 = f32[]{:T(128)} all-reduce(f32[]{:T(128)} %multiply_reduce_fusion.7), channel_id=1, replica_groups=mesh['col'=4,'row'=8] {'row','col'}, use_global_device_ids=true, to_apply=%region_4.0 | all-reduce | flops 1 | bytes 8 | tf_op jit(solution)/shard_map/psum | solution.py:14
  879.6 2.8 multiply_reduce_fusion.6
  882.4 39.8 %psum.65 = f32[]{:T(128)} all-reduce(f32[]{:T(128)} %multiply_reduce_fusion.6), channel_id=1, replica_groups=mesh['col'=4,'row'=8] {'row','col'}, use_global_device_ids=true, to_apply=%region_6.0 | all-reduce | flops 1 | bytes 8 | tf_op jit(solution)/shard_map/psum | solution.py:14
  922.9 3.0 broadcast_divide_fusion.3
  926.0 56.4 %all-gather.7.cloned.1.call-done = f32[2048,2,512]{0,2,1:T(8,128)} async-done(((f32[256,2,512]{0,2,1:T(8,128)}), f32[2048,2,512]{0,2,1:T(8,128)}) %all-gather.7.cloned.1.call-update) | async-done | bytes 8388624 | tf_op jit(solution)/shard_map/all_gather | solution.py:20
  982.4 103.3 %fusion.23 = f32[14,256,2,512,1]{1,3,0,2,4:T(8,128)} fusion(f32[2048,14,256,1]{2,0,1,3:T(8,128)} %bitcast.112, f32[2048,2,512]{0,2,1:T(8,128)} %all-gather.7.cloned.1.call-done), kind=kOutput, calls=%fused_computation.25 | convolution fusion | flops 90194313216 | bytes 52428800 | tf_op jit(solution)/shard_map/alc,asb->lcsb/dot_general | solution.py:21
  1085.7 19.5 copy.57
  1105.3 19.3 convolution_bitcast_fusion.2
  1124.6 114.4 %fusion.37 = f32[256,2,2048]{0,2,1:T(8,128)} fusion(f32[512,14,2048]{2,0,1:T(8,128)} %param.7, f32[256,512,14,2]{1,2,3,0:T(8,128)} %convolution_bitcast_fusion.2), kind=kOutput, calls=%fused_computation.29 | convolution fusion | flops 90194313216 | bytes 77594624 | tf_op jit(solution)/shard_map/cbrt,brd->ctd/dot_general | solution.py:23
  1239.1 76.8 %reduce-scatter.7.cloned.1.call-done = f32[256,2,512]{0,2,1:T(8,128)} async-done(((f32[256,2,2048]{0,2,1:T(8,128)}), f32[256,2,512]{0,2,1:T(8,128)}) %reduce-scatter.7.cloned.1.call-update) | async-done | bytes 1048592 | tf_op jit(solution)/shard_map/reduce_scatter | solution.py:24
  1315.9 2.1 multiply_reduce_fusion.5
  1318.0 40.5 %psum.66 = f32[]{:T(128)} all-reduce(f32[]{:T(128)} %multiply_reduce_fusion.5), channel_id=1, replica_groups=mesh['col'=4,'row'=8] {'row','col'}, use_global_device_ids=true, to_apply=%region_9.0 | all-reduce | flops 1 | bytes 8 | tf_op jit(solution)/shard_map/psum | solution.py:14
  1358.5 2.8 multiply_reduce_fusion.4
  1361.3 39.9 %psum.67 = f32[]{:T(128)} all-reduce(f32[]{:T(128)} %get-tuple-element.19), channel_id=1, replica_groups=mesh['col'=4,'row'=8] {'row','col'}, use_global_device_ids=true, to_apply=%region_11.0 | all-reduce | flops 1 | bytes 8 | tf_op jit(solution)/shard_map/psum | solution.py:14
  1403.0 56.4 %all-gather.9.cloned.1.call-done = f32[2048,2,512]{0,2,1:T(8,128)} async-done(((f32[256,2,512]{0,2,1:T(8,128)}), f32[2048,2,512]{0,2,1:T(8,128)}) %all-gather.9.cloned.1.call-update) | async-done | bytes 8388624 | tf_op jit(solution)/shard_map/all_gather | solution.py:20
  1459.4 103.3 %fusion.26 = f32[14,256,2,512,1]{1,3,0,2,4:T(8,128)} fusion(f32[2048,14,256,1]{2,0,1,3:T(8,128)} %bitcast.113, f32[2048,2,512]{0,2,1:T(8,128)} %all-gather.9.cloned.1.call-done), kind=kOutput, calls=%fused_computation.26 | convolution fusion | flops 90194313216 | bytes 52428800 | tf_op jit(solution)/shard_map/alc,asb->lcsb/dot_general | solution.py:21
  1562.8 19.5 copy.61
  1582.3 19.3 convolution_bitcast_fusion.1
  1601.6 114.4 %fusion.42 = f32[256,2,2048]{0,2,1:T(8,128)} fusion(f32[512,14,2048]{2,0,1:T(8,128)} %param.7, f32[256,512,14,2]{1,2,3,0:T(8,128)} %convolution_bitcast_fusion.1), kind=kOutput, calls=%fused_computation.30 | convolution fusion | flops 90194313216 | bytes 77594624 | tf_op jit(solution)/shard_map/cbrt,brd->ctd/dot_general | solution.py:23
  1716.1 76.8 %reduce-scatter.9.cloned.1.call-done = f32[256,2,512]{0,2,1:T(8,128)} async-done(((f32[256,2,2048]{0,2,1:T(8,128)}), f32[256,2,512]{0,2,1:T(8,128)}) %reduce-scatter.9.cloned.1.call-update) | async-done | bytes 1048592 | tf_op jit(solution)/shard_map/reduce_scatter | solution.py:24
  1792.9 2.1 multiply_reduce_fusion.3
  1795.0 40.5 %psum.68 = f32[]{:T(128)} all-reduce(f32[]{:T(128)} %multiply_reduce_fusion.3), channel_id=1, replica_groups=mesh['col'=4,'row'=8] {'row','col'}, use_global_device_ids=true, to_apply=%region_14.0 | all-reduce | flops 1 | bytes 8 | tf_op jit(solution)/shard_map/psum | solution.py:14
  1835.5 2.7 multiply_reduce_fusion.2
  1838.3 39.8 %psum.69 = f32[]{:T(128)} all-reduce(f32[]{:T(128)} %get-tuple-element.17), channel_id=1, replica_groups=mesh['col'=4,'row'=8] {'row','col'}, use_global_device_ids=true, to_apply=%region_16.0 | all-reduce | flops 1 | bytes 8 | tf_op jit(solution)/shard_map/psum | solution.py:14
  1879.9 56.4 %all-gather.11.cloned.1.call-done = f32[2048,2,512]{0,2,1:T(8,128)} async-done(((f32[256,2,512]{0,2,1:T(8,128)}), f32[2048,2,512]{0,2,1:T(8,128)}) %all-gather.11.cloned.1.call-update) | async-done | bytes 8388624 | tf_op jit(solution)/shard_map/all_gather | solution.py:20
  1936.3 103.3 %fusion.29 = f32[14,256,2,512,1]{1,3,0,2,4:T(8,128)} fusion(f32[2048,14,256,1]{2,0,1,3:T(8,128)} %bitcast.114, f32[2048,2,512]{0,2,1:T(8,128)} %all-gather.11.cloned.1.call-done), kind=kOutput, calls=%fused_computation.27 | convolution fusion | flops 90194313216 | bytes 52428800 | tf_op jit(solution)/shard_map/alc,asb->lcsb/dot_general | solution.py:21
  2039.7 19.5 copy.65
  2059.2 19.3 convolution_bitcast_fusion
  2078.5 114.3 %fusion.47 = f32[256,2,2048]{0,2,1:T(8,128)} fusion(f32[512,14,2048]{2,0,1:T(8,128)} %param.7, f32[256,512,14,2]{1,2,3,0:T(8,128)} %convolution_bitcast_fusion), kind=kOutput, calls=%fused_computation.31 | convolution fusion | flops 90194313216 | bytes 77594624 | tf_op jit(solution)/shard_map/cbrt,brd->ctd/dot_general | solution.py:23
  2192.9 76.8 %reduce-scatter.11.cloned.1.call-done = f32[256,2,512]{0,2,1:T(8,128)} async-done(((f32[256,2,2048]{0,2,1:T(8,128)}), f32[256,2,512]{0,2,1:T(8,128)}) %reduce-scatter.11.cloned.1.call-update) | async-done | bytes 1048592 | tf_op jit(solution)/shard_map/reduce_scatter | solution.py:24
  2269.7 2.1 multiply_reduce_fusion.1
  2271.8 40.5 %psum.70 = f32[]{:T(128)} all-reduce(f32[]{:T(128)} %multiply_reduce_fusion.1), channel_id=1, replica_groups=mesh['col'=4,'row'=8] {'row','col'}, use_global_device_ids=true, to_apply=%region_19.0 | all-reduce | flops 1 | bytes 8 | tf_op jit(solution)/shard_map/psum | solution.py:14
  2312.3 2.7 multiply_reduce_fusion
  2315.0 39.8 %psum.71 = f32[]{:T(128)} all-reduce(f32[]{:T(128)} %get-tuple-element.15), channel_id=1, replica_groups=mesh['col'=4,'row'=8] {'row','col'}, use_global_device_ids=true, to_apply=%region_21.0 | all-reduce | flops 1 | bytes 8 | tf_op jit(solution)/shard_map/psum | solution.py:14
  2355.6 1.3 copy.51
  2356.9 3.1 pad_maximum_fusion
  (30 shorter events, 5.2 us)
Async XLA Ops:
  40.4 7.3 copy-start.1
  40.4 408.4 %copy-start.2 = (f32[14,14,2,2]{1,3,2,0:T(2,128)S(1)}, f32[14,14,2,2]{1,3,2,0:T(2,128)}, u32[]{:S(2)}) copy-start(f32[14,14,2,2]{1,3,2,0:T(2,128)} %param.6) | copy-start | bytes 9412
  40.4 408.6 %all-to-all-start = ((f32[256,14,2048]{0,1,2:T(8,128)}), f32[256,14,2048]{0,1,2:T(8,128)}, u32[]{:S(2)}, u32[]{:S(2)}) async-start(f32[256,14,2048]{0,1,2:T(8,128)} %copy.32), calls=%async_computation | async-start | bytes 67108864 | tf_op jit(solution)/shard_map/all_to_all | solution.py:17
  47.6 456.0 %all-gather.5.cloned.1.call-start = ((), (), s32[]{:S(2)}) async-start(), calls=%async_computation.5 | async-start | bytes 9437184 | tf_op jit(solution)/shard_map/all_gather | solution.py:20
  448.6 388.4 %reduce-scatter.5.cloned.1.call-start = ((), (), s32[]{:S(2)}) async-start(), calls=%async_computation.6 | async-start | bytes 5242880 | tf_op jit(solution)/shard_map/reduce_scatter | solution.py:24
  760.2 222.2 %all-gather.7.cloned.1.call-start = ((), (), s32[]{:S(2)}) async-start(), calls=%async_computation.7 | async-start | bytes 9437184 | tf_op jit(solution)/shard_map/all_gather | solution.py:20
  925.9 390.0 %reduce-scatter.7.cloned.1.call-start = ((), (), s32[]{:S(2)}) async-start(), calls=%async_computation.8 | async-start | bytes 5242880 | tf_op jit(solution)/shard_map/reduce_scatter | solution.py:24
  1124.6 191.3 %copy-start = (f32[256,2,512]{0,2,1:T(8,128)S(1)}, f32[256,2,512]{0,2,1:T(8,128)}, u32[]{:S(2)}) copy-start(f32[256,2,512]{0,2,1:T(8,128)} %broadcast_divide_fusion.3) | copy-start | bytes 3145732
  1239.1 220.4 %all-gather.9.cloned.1.call-start = ((), (), s32[]{:S(2)}) async-start(), calls=%async_computation.9 | async-start | bytes 9437184 | tf_op jit(solution)/shard_map/all_gather | solution.py:20
  1403.0 390.0 %reduce-scatter.9.cloned.1.call-start = ((), (), s32[]{:S(2)}) async-start(), calls=%async_computation.10 | async-start | bytes 5242880 | tf_op jit(solution)/shard_map/reduce_scatter | solution.py:24
  1716.1 220.2 %all-gather.11.cloned.1.call-start = ((), (), s32[]{:S(2)}) async-start(), calls=%async_computation.11 | async-start | bytes 9437184 | tf_op jit(solution)/shard_map/all_gather | solution.py:20
  1879.9 389.8 %reduce-scatter.11.cloned.1.call-start = ((), (), s32[]{:S(2)}) async-start(), calls=%async_computation.12 | async-start | bytes 5242880 | tf_op jit(solution)/shard_map/reduce_scatter | solution.py:24
Sparse Core Ops, SparseCore 0:
  448.7 54.7 all-gather.4
  760.3 76.6 reduce-scatter.4
  926.1 56.3 all-gather.6
  1239.2 76.6 reduce-scatter.6
  1403.1 56.3 all-gather.8
  1716.2 76.6 reduce-scatter.8
  1880.0 56.3 all-gather.10
  2193.0 76.6 reduce-scatter.10
where the time goes:
time: 2370 us
  matrix products  948 us (40%)
  blocking collectives  718 us (30%)
  waiting for transfers between devices  498 us (21%)
  local copies, waits for them, and re-layouts  147 us (6%)
  other arithmetic  30.9 us (1%)
    psum x9, blocking collectives, global_dot(): return lax.psum(jnp.sum(left_vec * right_vec), all_axes)  718 us
    dot_general x4, matrix products, apply_ham(): jnp.einsum('cbrt,brd->ctd', t_two, right_blk, precision=EXACT_PREC, prefe...  458 us
    dot_general x4, matrix products, apply_ham(): jnp.einsum('alc,asb->lcsb', left_cols, vec_rows, precision=EXACT_PREC, pr...  413 us
    reduce_scatter x4, waiting for transfers between devices, apply_ham(): return lax.psum_scatter(y_part, 'col', scatter_dimension=2, tiled=True)  307 us
    all_gather x4, waiting for transfers between devices, apply_ham(): vec_rows = lax.all_gather(vec_blk, 'row', axis=0, tiled=True)  190 us
    dot_general x4, local copies, waits for them, and re-layouts, apply_ham(): jnp.einsum('alc,asb->lcsb', left_cols, vec_rows, precision=EXACT_PREC, pr...  78.1 us
    dot_general x4, matrix products, apply_ham(): jnp.einsum('lcsb,lrst->cbrt', t_one, mpo_tensor, precision=EXACT_PREC, pr...  77.2 us
  transfers between devices with their start and end apart: 9, of which 8 were waited for; matrix products, arithmetic and copies ran while one was open for 2% of the time, Pallas kernels for 0%

commit v1 on v0

v1 whole, which is shorter than its diff:
```python
import functools

import jax
import jax.numpy as jnp
from jax import lax
from jax.experimental import pallas as pl
from jax.experimental.pallas import tpu as pltpu
from jax.sharding import PartitionSpec as P

F32, BF16 = jnp.float32, jnp.bfloat16
STEPS = 4
NROW, NCOL = 8, 4
NDEV = NROW * NCOL
KRON = 8
PASSES = ((0, 3), (1, 2), (2, 1))


def div(a, b):
    return lax.div(a, jnp.int32(b))


def mod(a, b):
    return lax.rem(a, jnp.int32(b))


def split3(x):
    hi = x.astype(BF16)
    rest = x - hi.astype(F32)
    mid = rest.astype(BF16)
    low = (rest - mid.astype(F32)).astype(BF16)
    return hi, mid, low


def lanczos_kernel(ts, nd, psi, wk, lt, rt, out_v, out_ab,
                   vy, vcur, vprev, wprime, recv, t1, t2, l0, l1, l2, r0, r1, r2, vp, wkp, yacc, ar_src, ar_recv,
                   lsem, rsem, vsend, vrecv, ysend, yrecv, asend, arecv, iosem, fwd_ok, back_ok):
    row, col = lax.axis_index("row"), lax.axis_index("col")
    me = col * NROW + row
    core, xx, yy = mod(row, 2), mod(div(row, 2), 2), div(row, 4)
    per = nd // 2
    hs = ts // 2
    lps, rps = (l0, l1, l2), (r0, r1, r2)

    def six(lhs, rhs):
        a = [x for p, n in PASSES for x in lhs[:n]]
        b = [rhs[p] for p, n in PASSES for _ in range(n)]
        return jnp.dot(jnp.concatenate(a, axis=1), jnp.concatenate(b, axis=0), preferred_element_type=F32)

    def row_of(s):
        fc, fx, fy = mod(s, 2), mod(div(s, 2), 2), div(s, 4)
        c2, x2, y2 = core + fc - 2 * core * fc, xx + fx - 2 * xx * fx, yy + fy - 2 * yy * fy
        return (y2 * 2 + x2) * 2 + c2

    half_z = div(col, 2)
    zdir = 1 - 2 * half_z
    mz = col + half_z * (3 - 2 * col)

    def block_of(i):
        late, two, odd = div(i, 4), div(i, 2), mod(i, 2)
        d_in = (1 - late) * 3 * (1 - odd) + late * (4 - two)
        h_in = (1 - late) * two + late * odd
        return (1 - mz) * (3 - two) + mz * d_in, (1 - mz) * odd + mz * h_in

    def l_batch(g, hh, slot):
        a0 = pl.multiple_of(row_of(g) * ts, ts)
        a1 = pl.multiple_of(row_of(mod(g + hh, 8)) * ts, ts)
        base = per * slot
        if per > 1:
            pltpu.make_async_copy(lt.at[pl.ds(per * hh + 1, per - 1), :, pl.ds(a0, ts)],
                                  recv.at[pl.ds(base, per - 1)], lsem.at[slot]).start()
        pltpu.make_async_copy(lt.at[pl.ds(per - per * hh, 1), :, pl.ds(a1, ts)],
                              recv.at[pl.ds(base + per - 1, 1)], lsem.at[slot]).start()

    def l_batch_wait(slot):
        ref = recv.at[pl.ds(per * slot, per)]
        pltpu.make_async_copy(ref, ref, lsem.at[slot]).wait()

    def r_start(i):
        dm, h = block_of(i)
        dest = dm + half_z * (3 - 2 * dm)
        return pl.multiple_of((dest * 2 + h) * ts, ts)

    def r_batch(i, hh, slot):
        d0, d1 = r_start(i), r_start(mod(i + hh, 8))
        cols = pl.ds(pl.multiple_of(slot * ts, ts), ts)
        if per > 1:
            pltpu.make_async_copy(rt.at[pl.ds(4 * (per * hh + 1), 4 * per - 4), :, pl.ds(d0, ts)],
                                  t1.at[pl.ds(0, 4 * per - 4), pl.ds(0, hs), cols], rsem.at[slot]).start()
        pltpu.make_async_copy(rt.at[pl.ds(4 * (per - per * hh), 4), :, pl.ds(d1, ts)],
                              t1.at[pl.ds(4 * per - 4, 4), pl.ds(0, hs), cols], rsem.at[slot]).start()

    def r_batch_wait(slot):
        ref = t1.at[:, pl.ds(0, hs), pl.ds(pl.multiple_of(slot * ts, ts), ts)]
        pltpu.make_async_copy(ref, ref, rsem.at[slot]).wait()

    def pieces_of(k):
        return 0 if k == 0 else 2 - k % 2

    SB = min(32, ts)

    def l_split(slot, k, dst):
        for b in range(ts // SB):
            rows = pl.ds(b * SB, SB)
            for p, x in enumerate(split3(recv[per * slot + k, rows, :])):
                dst[p, rows, :] = x

    def r_split(slot, k, dst):
        cols = pl.ds(pl.multiple_of(slot * ts, ts), ts)
        sb = min(SB, hs)
        for kb in range(2):
            for bh in range(2):
                for b in range(hs // sb):
                    for p, x in enumerate(split3(t1[4 * k + 2 * kb + bh, pl.ds(b * sb, sb), cols])):
                        dst[p, kb, pl.ds(bh * hs + b * sb, sb), :] = x

    def ar_start(slot, tile):
        ar_src[slot] = tile
        ar_recv[slot, me] = tile

        def send(off, carry):
            to = mod(me + off, NDEV)
            pltpu.make_async_remote_copy(
                src_ref=ar_src.at[slot], dst_ref=ar_recv.at[slot, me], send_sem=asend.at[slot], recv_sem=arecv.at[slot],
                device_id={"col": div(to, NROW), "row": mod(to, NROW)}, device_id_type=pl.DeviceIdType.MESH).start()
            return carry

        lax.fori_loop(1, NDEV, send, 0)

    def ar_wait(slot):
        every = ar_recv.at[slot, pl.ds(0, NDEV - 1)]
        copy = pltpu.make_async_remote_copy(
            src_ref=every, dst_ref=every, send_sem=asend.at[slot], recv_sem=arecv.at[slot],
            device_id={"col": col, "row": row}, device_id_type=pl.DeviceIdType.MESH)
        copy.wait_send()
        copy.wait_recv()
        got = ar_recv[slot]
        first = lax.broadcasted_iota(jnp.int32, got.shape, 1) == 0
        return jnp.sum(jnp.where(first, got, 0.0)), jnp.max(jnp.where(first, 0.0, got))

    RB = min(64, ts)
    nblk = 4 * (ts // RB)

    def where_is(i):
        return div(i, ts // RB), pl.ds(pl.multiple_of(mod(i, ts // RB) * RB, RB), RB)

    def fold(op, x):
        x = x.reshape(RB // 8, 8, ts)
        y = x[0]
        for k in range(1, RB // 8):
            y = op(y, x[k])
        if ts <= 128:
            return y
        return op(y[:, :128], y[:, 128:])

    W8 = min(128, ts)

    def as_row(x, op):
        x = op(x, axis=0, keepdims=True)
        return x if W8 == 128 else jnp.concatenate([x, jnp.zeros((1, 128 - W8), F32)], axis=1)

    def two_rows(a, b):
        first = lax.broadcasted_iota(jnp.int32, (2, 128), 0) == 0
        return jnp.where(first, jnp.broadcast_to(a, (2, 128)), jnp.broadcast_to(b, (2, 128)))

    def vec(x):
        return jnp.full((8, 128), x, F32)

    def scaled_start(src_norm_coef):
        def scale(i, sq):
            n, rows = where_is(i)
            x = wprime[n, rows, :]
            vy[0, n, rows, :] = x * src_norm_coef
            return sq + fold(jnp.add, x * x)

        sq = lax.fori_loop(0, nblk, scale, jnp.zeros((8, W8), F32))
        ar_start(1, two_rows(as_row(sq, jnp.sum), jnp.zeros((1, 128), F32)))

    load = pltpu.make_async_copy(psi, wprime, iosem)
    load.start()
    l_first = pltpu.make_async_copy(lt.at[pl.ds(0, 1), :, pl.ds(pl.multiple_of(row * ts, ts), ts)],
                                    recv.at[pl.ds(2 * per - 1, 1)], lsem.at[1])
    l_first.start()
    r_first = pltpu.make_async_copy(rt.at[pl.ds(0, 4), :, pl.ds(r_start(jnp.int32(0)), ts)],
                                    t1.at[pl.ds(4 * per - 4, 4), pl.ds(0, hs), pl.ds(ts, ts)], rsem.at[1])
    r_first.start()
    zero_i = jnp.int32(0)
    l_batch(zero_i, zero_i, 0)
    for b in range(256 // 32):
        rows = pl.ds(b * 32, 32)
        for p, x in enumerate(split3(wk[rows, :])):
            wkp[p, rows, :] = x
    out_ab[...] = jnp.zeros_like(out_ab)

    load.wait()

    def biggest(i, mx):
        n, rows = where_is(i)
        x = wprime[n, rows, :]
        vprev[n, rows, :] = jnp.zeros((RB, ts), F32)
        return jnp.maximum(mx, fold(jnp.maximum, jnp.abs(x)))

    mx = lax.fori_loop(0, nblk, biggest, jnp.zeros((8, W8), F32))
    ar_start(0, two_rows(jnp.zeros((1, 128), F32), as_row(mx, jnp.max)))
    l_first.wait()
    l_split(1, per - 1, l0)
    r_first.wait()
    r_split(1, per - 1, r0)
    _, gmax = ar_wait(0)
    scaled_start(jnp.max(1.0 / vec(gmax)) * (2.0 ** -12))

    def v_copy(src, slot, s):
        return pltpu.make_async_remote_copy(
            src_ref=vy.at[src], dst_ref=vy.at[slot], send_sem=vsend.at[slot], recv_sem=vrecv.at[slot],
            device_id={"row": row_of(s)}, device_id_type=pl.DeviceIdType.MESH)

    def t1_chunk(pieces, l, keep):
        got = six([pieces[k] for k in range(3)], [vp[p] for p in range(3)])
        for n in range(4):
            at = (2 * l + n % 2, slice(None), pl.ds((n // 2) * ts, ts))
            t1[at] = jnp.where(keep, t1[at], 0.0) + got[:, n * ts:(n + 1) * ts]

    def t1_group(g, carry):
        @pl.when(g > 0)
        def _():
            v_copy(0, g, 0).wait_recv()

        @pl.when((g > 0) & (mod(g, 2) == 0))
        def _():
            v_copy(g, g + 1, 1).start()

        for n in range(4):
            for b in range(ts // SB):
                rows = pl.ds(b * SB, SB)
                for p, x in enumerate(split3(vy[g, n, rows, :])):
                    vp[p, rows, pl.ds(n * ts, ts)] = x

        def trip(hh, c2):
            @pl.when((g < 7) | (hh == 0))
            def _():
                l_batch(mod(g + hh, 8), 1 - hh, 1 - hh)

            l_batch_wait(hh)
            for k in range(per):
                l_split(hh, k, lps[pieces_of((k + 1) % per)])
                t1_chunk(lps[pieces_of(k)], per * hh + k, g > 0)
            return c2

        return lax.fori_loop(0, 2, trip, carry)

    t2_rows = min(64, hs)

    def t2_trip(factor, i, carry):
        c0 = pl.multiple_of(i * t2_rows, t2_rows)
        kron = 2 * nd * KRON
        for h in range(t2_rows // 16):
            parts = []
            for e in range(2):
                x = t1[:, pl.ds(c0 + h * 16 + e * 8, 8), :].reshape(kron, 2 * ts) * factor
                if kron < 256:
                    x = jnp.concatenate([x, jnp.zeros((256 - kron, 2 * ts), F32)], axis=0)
                got = six([wkp[k, pl.ds(0, kron), :] for k in range(3)], split3(x))
                parts.append(got.reshape(2 * nd, KRON, 2 * ts))
            for p, x in enumerate(split3(jnp.concatenate(parts, axis=1))):
                t2[p, :, pl.ds(c0 + h * 16, 16), :] = x
        return carry

    def y_copy(src, idx, slot, to):
        return pltpu.make_async_remote_copy(
            src_ref=src, dst_ref=landing(slot), send_sem=ysend.at[idx], recv_sem=yrecv.at[slot],
            device_id={"col": to}, device_id_type=pl.DeviceIdType.MESH)

    def y_ref(dm, h):
        return vy.at[4 + dm, pl.ds(2 * h, 2)]

    def landing(slot):
        return recv.at[pl.ds(2 * slot, 2)]

    def add_into(dm, h, slot):
        y_copy(landing(slot), 0, slot, col).wait_recv()

        def add(i, c):
            n, rows = where_is(i)
            vy[4 + dm, 2 * h + n, rows, :] = vy[4 + dm, 2 * h + n, rows, :] + recv[2 * slot + n, rows, :]
            return c

        lax.fori_loop(0, nblk // 2, add, 0)

    def t3_chunk(pieces, r):
        return six([t2[k, pl.ds(2 * r, 2), :, :].reshape(2 * ts, 2 * ts) for k in range(3)],
                   [pieces[k].reshape(2 * ts, ts) for k in range(3)])

    def t3_part(i, carry):
        dm, h = block_of(i)

        def trip(hh, c2):
            @pl.when((i < 7) | (hh == 0))
            def _():
                r_batch(mod(i + hh, 8), 1 - hh, 1 - hh)

            r_batch_wait(hh)
            total = None
            for k in range(per):
                r_split(hh, k, rps[pieces_of((k + 1) % per)])
                got = t3_chunk(rps[pieces_of(k)], per * hh + k)
                total = got if total is None else total + got
            yacc[...] = yacc[...] + total.reshape(2, ts, ts)
            return c2

        yacc[...] = jnp.zeros_like(yacc)
        lax.fori_loop(0, 2, trip, 0)
        vy[4 + dm, pl.ds(2 * h, 2)] = yacc[...]

        @pl.when(i == 2 * mz)
        def _():
            pl.semaphore_wait(fwd_ok, 1)

        @pl.when((mz == 1) & (i == 4))
        def _():
            pl.semaphore_wait(back_ok, 1)

        @pl.when((mz == 0) & (i < 6))
        def _():
            y_copy(y_ref(dm, h), i, i, col + zdir).start()

        @pl.when((mz == 1) & (i >= 2) & (i < 6))
        def _():
            k = i - 2
            add_into(3 - div(k, 2), mod(k, 2), k)
            y_copy(y_ref(3 - div(k, 2), mod(k, 2)), 6 + k, 6 + k, col + zdir).start()

        @pl.when((mz == 1) & (i >= 4) & (i < 6))
        def _():
            k = i - 4
            add_into(0, k, 6 + k)
            y_copy(y_ref(0, k), k, 6 + k, col - zdir).start()

        return carry

    def step(j, state):
        gmax, beta_prev = state
        for s in (1, 2, 4, 6):
            v_copy(0, s, s).start()
        lax.fori_loop(0, 8, t1_group, 0)
        for s in range(1, 8):
            v_copy(0, s, 0).wait_send()

        @pl.when(mz == 0)
        def _():
            pl.semaphore_signal(back_ok, inc=1, device_id={"col": col + zdir}, device_id_type=pl.DeviceIdType.MESH)

        @pl.when(mz == 1)
        def _():
            pl.semaphore_signal(fwd_ok, inc=1, device_id={"col": col + zdir}, device_id_type=pl.DeviceIdType.MESH)
            pl.semaphore_signal(fwd_ok, inc=1, device_id={"col": col - zdir}, device_id_type=pl.DeviceIdType.MESH)

        total, _ = ar_wait(1)
        norm_v = jnp.sqrt(vec(total))
        norm = jnp.max(norm_v)
        inv = jnp.max(1.0 / norm_v)
        factor = jnp.max(vec(gmax) / norm_v) * (2.0 ** 12)
        beta_prev = jnp.where(j > 0, norm, 0.0)
        lane = lax.broadcasted_iota(jnp.int32, (8, 128), 1)
        sub = lax.broadcasted_iota(jnp.int32, (8, 128), 0)
        out_ab[...] = jnp.where((sub == 1) & (lane == j - 1), norm_v, out_ab[...])

        lax.fori_loop(0, hs // t2_rows, functools.partial(t2_trip, factor), 0)
        r_batch(zero_i, zero_i, 0)
        lax.fori_loop(hs // t2_rows, ts // t2_rows, functools.partial(t2_trip, factor), 0)
        lax.fori_loop(0, 8, t3_part, 0)

        @pl.when(mz == 0)
        def _():
            for h in range(2):
                add_into(0, h, 6 + h)
            for k in range(6):
                y_copy(y_ref(0, 0), k, k, col).wait_send()

        @pl.when(mz == 1)
        def _():
            for h in range(2):
                add_into(1, h, 4 + h)
                add_into(1, h, 8 + h)
            for k in (0, 1, 6, 7, 8, 9):
                y_copy(y_ref(0, 0), k, k, col).wait_send()

        own = 4 + mz

        @pl.when(j < STEPS - 1)
        def _():
            l_batch(zero_i, zero_i, 0)

        def dots(i, c):
            n, rows = where_is(i)
            dot, mx = c
            w = vy[own, n, rows, :]
            v = wprime[n, rows, :] * inv
            vcur[n, rows, :] = v
            wprime[n, rows, :] = w
            return dot + fold(jnp.add, v * w), jnp.maximum(mx, fold(jnp.maximum, jnp.abs(w)))

        zero = jnp.zeros((8, W8), F32)
        dot, mx = lax.fori_loop(0, nblk, dots, (zero, zero))
        ar_start(0, two_rows(as_row(dot, jnp.sum), as_row(mx, jnp.max)))
        alpha, gmax = ar_wait(0)
        out_ab[...] = jnp.where((sub == 0) & (lane == j), vec(alpha), out_ab[...])
        small = jnp.max(1.0 / vec(gmax)) * (2.0 ** -12)

        def update(i, sq):
            n, rows = where_is(i)
            v = vcur[n, rows, :]
            x = wprime[n, rows, :] - alpha * v - beta_prev * vprev[n, rows, :]
            vprev[n, rows, :] = v
            wprime[n, rows, :] = x
            vy[0, n, rows, :] = x * small
            return sq + fold(jnp.add, x * x)

        sq = lax.fori_loop(0, nblk, update, zero)
        ar_start(1, two_rows(as_row(sq, jnp.sum), jnp.zeros((1, 128), F32)))
        return gmax, norm

    lax.fori_loop(0, STEPS, step, (gmax, jnp.float32(0)))

    total, _ = ar_wait(1)
    norm_v = jnp.sqrt(vec(total))
    inv = jnp.max(1.0 / norm_v)
    lane = lax.broadcasted_iota(jnp.int32, (8, 128), 1)
    sub = lax.broadcasted_iota(jnp.int32, (8, 128), 0)
    out_ab[...] = jnp.where((sub == 1) & (lane == STEPS - 1), norm_v, out_ab[...])

    def last(i, c):
        n, rows = where_is(i)
        wprime[n, rows, :] = wprime[n, rows, :] * inv
        return c

    lax.fori_loop(0, nblk, last, 0)
    store = pltpu.make_async_copy(wprime, out_v, iosem)
    store.start()
    store.wait()


def local_steps(ts, nd, psi_blk, left_blk, mpo_tensor, right_blk):
    psi = psi_blk.reshape(ts, 2, 2, ts).transpose(2, 1, 0, 3).reshape(4, ts, ts)
    lt = left_blk.transpose(1, 0, 2)
    rt = right_blk.transpose(1, 0, 2).reshape(4 * nd, ts // 2, 8 * ts)
    w2 = mpo_tensor.transpose(1, 3, 0, 2).reshape(2 * nd, 1, 2 * nd, 1)
    eye = jnp.eye(KRON, dtype=F32).reshape(1, KRON, 1, KRON)
    wk = (w2 * eye).reshape(2 * nd * KRON, 2 * nd * KRON)
    pad = 256 - 2 * nd * KRON
    wk = jnp.pad(wk, ((0, pad), (0, pad)))
    any_space = pl.BlockSpec(memory_space=pl.ANY)
    vmem = pl.BlockSpec(memory_space=pltpu.VMEM)
    dma, V = pltpu.SemaphoreType.DMA, pltpu.VMEM
    out_v, out_ab = pl.pallas_call(
        functools.partial(lanczos_kernel, ts, nd),
        out_shape=(jax.ShapeDtypeStruct((4, ts, ts), F32), jax.ShapeDtypeStruct((8, 128), F32)),
        in_specs=[any_space, vmem, any_space, any_space],
        out_specs=(any_space, vmem),
        scratch_shapes=[
            V((8, 4, ts, ts), F32), V((4, ts, ts), F32), V((4, ts, ts), F32), V((4, ts, ts), F32),
            V((20, ts, ts), F32), V((2 * nd, ts, 2 * ts), F32), V((3, 2 * nd, ts, 2 * ts), BF16),
            V((3, ts, ts), BF16), V((3, ts, ts), BF16), V((3, ts, ts), BF16),
            V((3, 2, ts, ts), BF16), V((3, 2, ts, ts), BF16), V((3, 2, ts, ts), BF16),
            V((3, ts, 4 * ts), BF16), V((3, 256, 256), BF16), V((2, ts, ts), F32),
            V((2, 2, 128), F32), V((2, NDEV, 2, 128), F32),
            dma((2,)), dma((2,)), dma((8,)), dma((8,)), dma((10,)), dma((10,)), dma((2,)), dma((2,)), dma,
            pltpu.SemaphoreType.REGULAR, pltpu.SemaphoreType.REGULAR,
        ],
        compiler_params=pltpu.CompilerParams(vmem_limit_bytes=67043328, has_side_effects=True),
    )(psi, wk, lt, rt)
    v_next = out_v.reshape(2, 2, ts, ts).transpose(2, 1, 0, 3).reshape(ts, 2, 2 * ts)
    return out_ab[0, :STEPS], out_ab[1, :STEPS], v_next


def build(mesh, ts, nd):
    return jax.shard_map(
        functools.partial(local_steps, ts, nd), mesh=mesh,
        in_specs=(P("row", None, "col"), P("row", None, None), P(), P("col", None, None)),
        out_specs=(P(), P(), P("row", None, "col")), check_vma=False)


def solution(mesh):
    return build(mesh, 256, 14)
```

time: 2370 us -> 898 us (0.38)
  matrix products: 948 us -> 0 us
  Pallas kernels: 0 us -> 882 us
  blocking collectives: 718 us -> 0 us
  waiting for transfers between devices: 498 us -> 0 us
  local copies, waits for them, and re-layouts: 147 us -> 13.3 us
  other arithmetic: 30.9 us -> 2.33 us
    dot_general x12 -> x0, matrix products: 948 us -> none  [the longest x4 458 us: apply_ham(): jnp.einsum('cbrt,brd->ctd', t_two, right_blk, precision=EXACT_PREC, prefe...]
    pallas_call x0 -> x1, Pallas kernels: none -> 882 us  [local_steps(): pl.pallas_call(functools.partial(lanczos_kernel, ts, nd), out_shape=(jax....]
    psum x9 -> x0, blocking collectives: 718 us -> none  [global_dot(): return lax.psum(jnp.sum(left_vec * right_vec), all_axes)]
    reduce_scatter x4 -> x0, waiting for transfers between devices: 307 us -> none  [apply_ham(): return lax.psum_scatter(y_part, 'col', scatter_dimension=2, tiled=True)]
    all_gather x4 -> x0, waiting for transfers between devices: 190 us -> none  [apply_ham(): vec_rows = lax.all_gather(vec_blk, 'row', axis=0, tiled=True)]
    dot_general x4 -> x0, local copies, waits for them, and re-layouts: 78.1 us -> none  [apply_ham(): jnp.einsum('alc,asb->lcsb', left_cols, vec_rows, precision=EXACT_PREC, pr...]
    unnamed x10 -> x2, local copies, waits for them, and re-layouts: 35.3 us -> 0.01 us
    all_to_all x1 -> x0, local copies, waits for them, and re-layouts: 33.5 us -> none  [local_steps(): left_cols = lax.all_to_all(left_blk, 'row', 2, 0, tiled=True)]
  transfers between devices with their start and end apart: 9 -> 0, of which waited for: 8 -> 0; matrix products, arithmetic and copies ran while one was open for 2% -> 0% of each run, Pallas kernels for 0% -> 0%
where the time goes in v1:
time: 898 us
  Pallas kernels  882 us (98%)
  local copies, waits for them, and re-layouts  13.3 us (1%)
    pallas_call x1, Pallas kernels, local_steps(): pl.pallas_call(functools.partial(lanczos_kernel, ts, nd), out_shape=(jax....  882 us

profile of v1, /device:TPU:0, one launch (start us, length us, event | category | flops | bytes accessed | tf_op | source)
XLA Modules:
  0.0 898.1 jit_solution(2737856932240588913)
XLA Ops:
  0.6 1.1 copy.10
  1.7 0.1 mul.19
  1.9 0.0 copy-start
  1.9 2.3 broadcast_multiply_fusion
  4.2 3.5 mul.23
  7.7 0.7 pad.4.wk
  8.4 0.0 copy-done
  8.4 1.2 reshape.36
  9.6 1.2 copy.9
  10.8 881.8 %shard_map.67 = (f32[4,256,256]{2,1,0:T(8,128)}, f32[8,128]{1,0:T(8,128)}) custom-call(f32[4,256,256]{2,1,0:T(8,128)} %bitcast.17, f32[256,256]{1,0:T(8,128)} %pad.4.wk, f32[14,256,2048]{2,1,0:T(8,128)} %bitcast.16, f32[56,128,2048]{2,1,0:T(8,128)} %bitcast.15), custom_call_target="tpu_custom_call" | custom-call | tf_op jit(solution)/shard_map/pallas_call | solution.py:453
  892.6 1.3 slice_bitcast_fusion
  893.9 2.0 copy.11
  895.9 2.2 reshape.40
  (1 shorter events, 0.0 us)
Async XLA Ops:
  1.9 6.5 copy-start

commit v2 on v1

v2 whole, which is shorter than its diff:
```python
import functools

import jax
import jax.numpy as jnp
from jax import lax
from jax.experimental import pallas as pl
from jax.experimental.pallas import tpu as pltpu
from jax.sharding import PartitionSpec as P

F32, BF16 = jnp.float32, jnp.bfloat16
STEPS = 4
NROW, NCOL = 8, 4
NDEV = NROW * NCOL
KRON = 4
PASSES = ((0, 3), (1, 2), (2, 1))


def div(a, b):
    return lax.div(a, jnp.int32(b))


def mod(a, b):
    return lax.rem(a, jnp.int32(b))


def split3(x):
    hi = x.astype(BF16)
    rest = x - hi.astype(F32)
    mid = rest.astype(BF16)
    low = (rest - mid.astype(F32)).astype(BF16)
    return hi, mid, low


def lanczos_kernel(ts, nd, psi, w2, lt, rt, out_v, out_a, out_b,
                   psi_v, vy, vcur, vprev, wprime, recv, t1, t2, l0, l1, r0, r1, vp, wk6, ar_src, ar_recv,
                   lsem, rsem, vsend, vrecv, ysend, yrecv, asend, arecv, iosem, fwd_ok, back_ok):
    row, col = lax.axis_index("row"), lax.axis_index("col")
    me = col * NROW + row
    core, xx, yy = mod(row, 2), mod(div(row, 2), 2), div(row, 4)
    hs = ts // 2
    kron = 2 * nd * KRON
    lps, rps = (l0, l1), (r0, r1)

    def six(lhs, rhs):
        a = [x for p, n in PASSES for x in lhs[:n]]
        b = [rhs[p] for p, n in PASSES for _ in range(n)]
        return jnp.dot(jnp.concatenate(a, axis=1), jnp.concatenate(b, axis=0), preferred_element_type=F32)

    def row_of(s):
        hi, two, odd = div(s, 4), mod(div(s, 2), 2), mod(s, 2)
        fp = (1 - hi) * two * (1 - odd) + hi * (two + (1 - two) * odd)
        fq = (1 - hi) * two * odd + hi * (two + (1 - two) * (1 - odd))
        fx, fy = (1 - core) * fp + core * fq, (1 - core) * fq + core * fp
        c2, x2, y2 = core + odd - 2 * core * odd, xx + fx - 2 * xx * fx, yy + fy - 2 * yy * fy
        return (y2 * 2 + x2) * 2 + c2

    half_z = div(col, 2)
    zdir = 1 - 2 * half_z
    mz = col + half_z * (3 - 2 * col)

    def block_of(i):
        late, two, odd = div(i, 4), div(i, 2), mod(i, 2)
        d_in = (1 - late) * 3 * (1 - odd) + late * (4 - two)
        h_in = (1 - late) * two + late * odd
        return (1 - mz) * (3 - two) + mz * d_in, (1 - mz) * odd + mz * h_in

    def l_batch(g):
        slot = mod(g, 2)
        a0 = pl.multiple_of(row_of(g) * ts, ts)
        a1 = pl.multiple_of(row_of(mod(g + 1, 8)) * ts, ts)
        pltpu.make_async_copy(lt.at[pl.ds(1, nd - 1), :, pl.ds(a0, ts)],
                              recv.at[pl.ds(nd * slot, nd - 1)], lsem.at[slot]).start()
        pltpu.make_async_copy(lt.at[pl.ds(0, 1), :, pl.ds(a1, ts)],
                              recv.at[pl.ds(nd * slot + nd - 1, 1)], lsem.at[slot]).start()

    def l_batch_wait(slot):
        ref = recv.at[pl.ds(nd * slot, nd)]
        pltpu.make_async_copy(ref, ref, lsem.at[slot]).wait()

    def r_start(i):
        dm, h = block_of(i)
        dest = dm + half_z * (3 - 2 * dm)
        return pl.multiple_of((dest * 2 + h) * ts, ts)

    def r_rows(slot):
        return pl.ds(pl.multiple_of(slot * hs, hs), hs)

    half = nd // 2

    def r_batch(i):
        slot = mod(i, 2)
        d0, d1 = r_start(i), r_start(mod(i + 1, 8))
        for first, count, d, hh, plane in ((1, half, d0, 0, 0), (half + 1, half - 1, d0, 1, 0), (0, 1, d1, 1, 4 * half - 4)):
            if count:
                pltpu.make_async_copy(rt.at[pl.ds(4 * first, 4 * count), :, pl.ds(d, ts)],
                                      t1.at[pl.ds(plane, 4 * count), r_rows(slot), pl.ds(hh * ts, ts)],
                                      rsem.at[slot]).start()

    def r_batch_wait(slot):
        ref = t1.at[pl.ds(0, 4 * half), r_rows(slot)]
        pltpu.make_async_copy(ref, ref, rsem.at[slot]).wait()

    SB = min(32, ts)

    def l_split(slot, k, dst):
        for b in range(ts // SB):
            rows = pl.ds(b * SB, SB)
            for p, x in enumerate(split3(recv[nd * slot + k, rows, :])):
                dst[p, rows, :] = x

    def r_split(slot, k, dst):
        hh, kk = k // half, k % half
        sb = min(SB, hs)
        for kb in range(2):
            for bh in range(2):
                for b in range(hs // sb):
                    rows = pl.ds(pl.multiple_of(slot * hs + b * sb, sb), sb)
                    for p, x in enumerate(split3(t1[4 * kk + 2 * kb + bh, rows, pl.ds(hh * ts, ts)])):
                        dst[p, kb, pl.ds(bh * hs + b * sb, sb), :] = x

    def ar_start(slot, tile):
        ar_src[slot] = tile
        ar_recv[slot, me] = tile

        def send(off, carry):
            to = mod(me + off, NDEV)
            pltpu.make_async_remote_copy(
                src_ref=ar_src.at[slot], dst_ref=ar_recv.at[slot, me], send_sem=asend.at[slot], recv_sem=arecv.at[slot],
                device_id={"col": div(to, NROW), "row": mod(to, NROW)}, device_id_type=pl.DeviceIdType.MESH).start()
            return carry

        lax.fori_loop(1, NDEV, send, 0)

    def ar_wait(slot):
        every = ar_recv.at[slot, pl.ds(0, NDEV - 1)]
        copy = pltpu.make_async_remote_copy(
            src_ref=every, dst_ref=every, send_sem=asend.at[slot], recv_sem=arecv.at[slot],
            device_id={"col": col, "row": row}, device_id_type=pl.DeviceIdType.MESH)
        copy.wait_send()
        copy.wait_recv()
        got = ar_recv[slot]
        first = lax.broadcasted_iota(jnp.int32, got.shape, 1) == 0
        return jnp.sum(jnp.where(first, got, 0.0)), jnp.max(jnp.where(first, 0.0, got))

    RB = min(64, ts)
    nblk = 4 * (ts // RB)

    def where_is(i):
        return div(i, ts // RB), pl.ds(pl.multiple_of(mod(i, ts // RB) * RB, RB), RB)

    def fold(op, x):
        x = x.reshape(RB // 8, 8, ts)
        y = x[0]
        for k in range(1, RB // 8):
            y = op(y, x[k])
        if ts <= 128:
            return y
        return op(y[:, :128], y[:, 128:])

    W8 = min(128, ts)

    def as_row(x, op):
        x = op(x, axis=0, keepdims=True)
        return x if W8 == 128 else jnp.concatenate([x, jnp.zeros((1, 128 - W8), F32)], axis=1)

    def two_rows(a, b):
        first = lax.broadcasted_iota(jnp.int32, (2, 128), 0) == 0
        return jnp.where(first, jnp.broadcast_to(a, (2, 128)), jnp.broadcast_to(b, (2, 128)))

    def vec(x):
        return jnp.full((8, 128), x, F32)

    def scaled_start(src_norm_coef):
        def scale(i, sq):
            n, rows = where_is(i)
            x = wprime[n, rows, :]
            vy[0, n, rows, :] = x * src_norm_coef
            return sq + fold(jnp.add, x * x)

        sq = lax.fori_loop(0, nblk, scale, jnp.zeros((8, W8), F32))
        ar_start(1, two_rows(as_row(sq, jnp.sum), jnp.zeros((1, 128), F32)))

    LB = min(128, ts)
    blocks = range(2 * ts // LB)
    loads = [pltpu.make_async_copy(psi.at[:, pl.ds(b * LB, LB)], psi_v.at[b], iosem.at[b]) for b in blocks]
    for load in loads:
        load.start()
    l_first = pltpu.make_async_copy(lt.at[pl.ds(0, 1), :, pl.ds(pl.multiple_of(row * ts, ts), ts)],
                                    recv.at[pl.ds(2 * nd - 1, 1)], lsem.at[1])
    l_first.start()
    zero_i = jnp.int32(0)
    r_first = pltpu.make_async_copy(rt.at[pl.ds(0, 4), :, pl.ds(r_start(zero_i), ts)],
                                    t1.at[pl.ds(4 * half - 4, 4), r_rows(1), pl.ds(ts, ts)], rsem.at[1])
    r_first.start()
    l_batch(zero_i)
    for b, load in enumerate(loads):
        load.wait()
        for sp in range(2):
            wprime[2 * (b * LB // ts) + sp, :, pl.ds(b * LB % ts, LB)] = psi_v[b, pl.ds(sp, ts, stride=2), :]

    def biggest(i, mx):
        n, rows = where_is(i)
        x = wprime[n, rows, :]
        vprev[n, rows, :] = jnp.zeros((RB, ts), F32)
        return jnp.maximum(mx, fold(jnp.maximum, jnp.abs(x)))

    mx = lax.fori_loop(0, nblk, biggest, jnp.zeros((8, W8), F32))
    ar_start(0, two_rows(jnp.zeros((1, 128), F32), as_row(mx, jnp.max)))
    pieces = split3(w2[...])
    up = (div(lax.broadcasted_iota(jnp.int32, (kron, 2 * nd), 0), KRON)
          == lax.broadcasted_iota(jnp.int32, (kron, 2 * nd), 1)).astype(F32).astype(BF16)
    lane = lax.broadcasted_iota(jnp.int32, (2 * nd, 6 * kron), 1)
    across = (div(mod(lane, kron), KRON) == lax.broadcasted_iota(jnp.int32, (2 * nd, 6 * kron), 0)).astype(F32).astype(BF16)
    lane = lax.broadcasted_iota(jnp.int32, (kron, 6 * kron), 1)
    same = mod(lane, KRON) == mod(lax.broadcasted_iota(jnp.int32, (kron, 6 * kron), 0), KRON)
    which = div(lane, kron)
    total = jnp.zeros((kron, 6 * kron), F32)
    for k in range(3):
        tall = jnp.dot(up, pieces[k], preferred_element_type=F32).astype(BF16)
        wide = jnp.dot(tall, across, preferred_element_type=F32)
        here = [n for n, kk in enumerate(kk for p, n2 in PASSES for kk in range(n2)) if kk == k]
        mask = same & functools.reduce(jnp.logical_or, [which == n for n in here])
        total = jnp.where(mask, wide, total)
    wk6[...] = total.astype(BF16)
    l_first.wait()
    l_split(1, nd - 1, l0)
    r_first.wait()
    r_split(1, nd - 1, r0)
    _, gmax = ar_wait(0)
    scaled_start(jnp.max(1.0 / vec(gmax)) * (2.0 ** -12))

    def v_copy(src, slot, s):
        return pltpu.make_async_remote_copy(
            src_ref=vy.at[src], dst_ref=vy.at[slot], send_sem=vsend.at[slot], recv_sem=vrecv.at[slot],
            device_id={"row": row_of(s)}, device_id_type=pl.DeviceIdType.MESH)

    def swap(a, b):
        a, b = a.reshape(-1, 8, a.shape[-1]), b.reshape(-1, 8, b.shape[-1])
        low = lax.broadcasted_iota(jnp.int32, a.shape, 1) < 4
        return jnp.where(low, a, pltpu.roll(b, 4, 1)), jnp.where(low, pltpu.roll(a, 4, 1), b)

    def t1_chunk(pieces, l, keep):
        got = six([pieces[k] for k in range(3)], [vp[p] for p in range(3)])
        for bh in range(2):
            both = swap(got[:, 2 * bh * ts:(2 * bh + 1) * ts], got[:, (2 * bh + 1) * ts:(2 * bh + 2) * ts])
            for e in range(2):
                at = (2 * l + e, slice(None), pl.ds(bh * ts, ts))
                t1[at] = jnp.where(keep, t1[at], 0.0) + both[e].reshape(ts, ts)

    def t1_group(g, carry):
        @pl.when(g > 0)
        def _():
            v_copy(0, g, 0).wait_recv()

        @pl.when((g > 0) & (mod(g, 2) == 0))
        def _():
            v_copy(g, g + 1, 1).start()

        @pl.when((g == 1) | (g == 2))
        def _():
            v_copy(0, 2 + 2 * g, 2 + 2 * g).start()

        @pl.when(g < 7)
        def _():
            l_batch(g + 1)

        slot = mod(g, 2)
        l_batch_wait(slot)
        for n in range(4):
            for b in range(ts // SB):
                rows = pl.ds(b * SB, SB)
                for p, x in enumerate(split3(vy[g, n, rows, :])):
                    vp[p, rows, pl.ds(n * ts, ts)] = x
        for k in range(nd):
            l_split(slot, k, lps[(k + 1) % 2])
            t1_chunk(lps[k % 2], k, g > 0)
        return carry

    t2_rows = min(64, hs)

    def t2_trip(i, carry):
        @pl.when(i == (hs // t2_rows))
        def _():
            r_batch(zero_i)

        c0 = pl.multiple_of(i * t2_rows, t2_rows)
        for h in range(t2_rows // 8):
            x = t1[:, pl.ds(c0 + h * 8, 8), :].reshape(nd, 2, 8, 2 * ts)
            parts = []
            for e in range(2):
                b = split3(x[:, e].reshape(kron, 2 * ts))
                rhs = jnp.concatenate([b[p] for p, n in PASSES for _ in range(n)], axis=0)
                got = jnp.dot(wk6[...], rhs, preferred_element_type=F32)
                parts.append(got.reshape(nd, 8, 2 * ts))
            for p, y in enumerate(split3(jnp.concatenate(parts, axis=1))):
                t2[p, :, pl.ds(2 * c0 + h * 16, 16), :] = y
        return carry

    def y_copy(src, idx, slot, to):
        return pltpu.make_async_remote_copy(
            src_ref=src, dst_ref=landing(slot), send_sem=ysend.at[idx], recv_sem=yrecv.at[slot],
            device_id={"col": to}, device_id_type=pl.DeviceIdType.MESH)

    def y_ref(dm, h):
        return vy.at[4 + dm, pl.ds(2 * h, 2)]

    def landing(slot):
        return recv.at[pl.ds(2 * slot, 2)]

    def add_into(dm, h, slot):
        y_copy(landing(slot), 0, slot, col).wait_recv()

        def add(i, c):
            n, rows = where_is(i)
            vy[4 + dm, 2 * h + n, rows, :] = vy[4 + dm, 2 * h + n, rows, :] + recv[2 * slot + n, rows, :]
            return c

        lax.fori_loop(0, nblk // 2, add, 0)

    def t3_chunk(pieces, r):
        return six([t2[k, r] for k in range(3)],
                   [pieces[k].reshape(2 * ts, ts) for k in range(3)])

    def t3_part(factor, i, carry):
        dm, h = block_of(i)

        @pl.when(i < 7)
        def _():
            r_batch(i + 1)

        slot = mod(i, 2)
        r_batch_wait(slot)
        total = None
        for k in range(nd):
            r_split(slot, k, rps[(k + 1) % 2])
            got = t3_chunk(rps[k % 2], k)
            total = got if total is None else total + got
        total = (total * factor).reshape(ts // 8, 16, ts)
        for e, y in enumerate(swap(total[:, :8], total[:, 8:])):
            vy[4 + dm, 2 * h + e] = y.reshape(ts, ts)

        @pl.when(i == 2 * mz)
        def _():
            pl.semaphore_wait(fwd_ok, 1)

        @pl.when((mz == 1) & (i == 4))
        def _():
            pl.semaphore_wait(back_ok, 1)

        @pl.when((mz == 0) & (i < 6))
        def _():
            y_copy(y_ref(dm, h), i, i, col + zdir).start()

        @pl.when((mz == 1) & (i >= 2) & (i < 6))
        def _():
            k = i - 2
            add_into(3 - div(k, 2), mod(k, 2), k)
            y_copy(y_ref(3 - div(k, 2), mod(k, 2)), 6 + k, 6 + k, col + zdir).start()

        @pl.when((mz == 1) & (i >= 4) & (i < 6))
        def _():
            k = i - 4
            add_into(0, k, 6 + k)
            y_copy(y_ref(0, k), k, 6 + k, col - zdir).start()

        return carry

    def step(j, state):
        gmax, beta_prev = state
        for s in (1, 2):
            v_copy(0, s, s).start()
        lax.fori_loop(0, 8, t1_group, 0)
        for s in range(1, 8):
            v_copy(0, s, 0).wait_send()

        @pl.when(mz == 0)
        def _():
            pl.semaphore_signal(back_ok, inc=1, device_id={"col": col + zdir}, device_id_type=pl.DeviceIdType.MESH)

        @pl.when(mz == 1)
        def _():
            pl.semaphore_signal(fwd_ok, inc=1, device_id={"col": col + zdir}, device_id_type=pl.DeviceIdType.MESH)
            pl.semaphore_signal(fwd_ok, inc=1, device_id={"col": col - zdir}, device_id_type=pl.DeviceIdType.MESH)

        total, _ = ar_wait(1)
        norm_v = jnp.sqrt(vec(total))
        norm = jnp.max(norm_v)
        inv = jnp.max(1.0 / norm_v)
        factor = jnp.max(vec(gmax) / norm_v) * (2.0 ** 12)
        beta_prev = jnp.where(j > 0, norm, 0.0)

        @pl.when(j > 0)
        def _():
            out_b[j - 1] = norm

        lax.fori_loop(0, ts // t2_rows, t2_trip, 0)
        lax.fori_loop(0, 8, functools.partial(t3_part, factor), 0)

        @pl.when(mz == 0)
        def _():
            for h in range(2):
                add_into(0, h, 6 + h)
            for k in range(6):
                y_copy(y_ref(0, 0), k, k, col).wait_send()

        @pl.when(mz == 1)
        def _():
            for h in range(2):
                add_into(1, h, 4 + h)
                add_into(1, h, 8 + h)
            for k in (0, 1, 6, 7, 8, 9):
                y_copy(y_ref(0, 0), k, k, col).wait_send()

        own = 4 + mz

        @pl.when(j < STEPS - 1)
        def _():
            l_batch(zero_i)

        def dots(i, c):
            n, rows = where_is(i)
            dot, mx = c
            w = vy[own, n, rows, :]
            v = wprime[n, rows, :] * inv
            vcur[n, rows, :] = v
            wprime[n, rows, :] = w
            return dot + fold(jnp.add, v * w), jnp.maximum(mx, fold(jnp.maximum, jnp.abs(w)))

        zero = jnp.zeros((8, W8), F32)
        dot, mx = lax.fori_loop(0, nblk, dots, (zero, zero))
        ar_start(0, two_rows(as_row(dot, jnp.sum), as_row(mx, jnp.max)))
        alpha, gmax = ar_wait(0)
        out_a[j] = alpha
        small = jnp.max(1.0 / vec(gmax)) * (2.0 ** -12)

        def update(i, sq):
            n, rows = where_is(i)
            v = vcur[n, rows, :]
            x = wprime[n, rows, :] - alpha * v - beta_prev * vprev[n, rows, :]
            vprev[n, rows, :] = v
            wprime[n, rows, :] = x
            vy[0, n, rows, :] = x * small
            return sq + fold(jnp.add, x * x)

        sq = lax.fori_loop(0, nblk, update, zero)
        ar_start(1, two_rows(as_row(sq, jnp.sum), jnp.zeros((1, 128), F32)))
        return gmax, norm

    lax.fori_loop(0, STEPS, step, (gmax, jnp.float32(0)))

    total, _ = ar_wait(1)
    norm_v = jnp.sqrt(vec(total))
    inv = jnp.max(1.0 / norm_v)
    out_b[STEPS - 1] = jnp.max(norm_v)

    stores = [pltpu.make_async_copy(psi_v.at[b], out_v.at[:, pl.ds(b * LB, LB)], iosem.at[b]) for b in blocks]
    for b, store in enumerate(stores):
        for sp in range(2):
            psi_v[b, pl.ds(sp, ts, stride=2), :] = wprime[2 * (b * LB // ts) + sp, :, pl.ds(b * LB % ts, LB)] * inv
        store.start()
    for store in stores:
        store.wait()


def local_steps(ts, nd, psi_blk, left_blk, mpo_tensor, right_blk):
    psi = psi_blk.reshape(2 * ts, 2 * ts)
    lt = left_blk.transpose(1, 0, 2)
    rt = right_blk.transpose(1, 0, 2).reshape(4 * nd, ts // 2, 8 * ts)
    w2 = mpo_tensor.transpose(1, 3, 0, 2).reshape(2 * nd, 2 * nd)
    any_space = pl.BlockSpec(memory_space=pl.ANY)
    vmem = pl.BlockSpec(memory_space=pltpu.VMEM)
    dma, V = pltpu.SemaphoreType.DMA, pltpu.VMEM
    smem = pl.BlockSpec(memory_space=pltpu.SMEM)
    out_v, alpha, beta = pl.pallas_call(
        functools.partial(lanczos_kernel, ts, nd),
        out_shape=(jax.ShapeDtypeStruct((2 * ts, 2 * ts), F32),) + (jax.ShapeDtypeStruct((STEPS,), F32),) * 2,
        in_specs=[any_space, vmem, any_space, any_space],
        out_specs=(any_space, smem, smem),
        scratch_shapes=[
            V((2 * ts // min(128, ts), 2 * ts, min(128, ts)), F32), V((8, 4, ts, ts), F32), V((4, ts, ts), F32), V((4, ts, ts), F32), V((4, ts, ts), F32),
            V((max(20, 2 * nd), ts, ts), F32), V((2 * nd, ts, 2 * ts), F32), V((3, nd, 2 * ts, 2 * ts), BF16),
            V((3, ts, ts), BF16), V((3, ts, ts), BF16), V((3, 2, ts, ts), BF16), V((3, 2, ts, ts), BF16),
            V((3, ts, 4 * ts), BF16), V((2 * nd * KRON, 12 * nd * KRON), BF16),
            V((2, 2, 128), F32), V((2, NDEV, 2, 128), F32),
            dma((2,)), dma((2,)), dma((8,)), dma((8,)), dma((10,)), dma((10,)), dma((2,)), dma((2,)), dma((4,)),
            pltpu.SemaphoreType.REGULAR, pltpu.SemaphoreType.REGULAR,
        ],
        compiler_params=pltpu.CompilerParams(vmem_limit_bytes=67043328, has_side_effects=True),
    )(psi, w2, lt, rt)
    return alpha, beta, out_v.reshape(ts, 2, 2 * ts)


def build(mesh, ts, nd):
    return jax.shard_map(
        functools.partial(local_steps, ts, nd), mesh=mesh,
        in_specs=(P("row", None, "col"), P("row", None, None), P(), P("col", None, None)),
        out_specs=(P(), P(), P("row", None, "col")), check_vma=False)


def solution(mesh):
    return build(mesh, 256, 14)
```

time: 898 us -> 849 us (0.945)
  Pallas kernels: 882 us -> 838 us
    pallas_call x1, Pallas kernels: 882 us -> 838 us  [local_steps(): pl.pallas_call(functools.partial(lanczos_kernel, ts, nd), out_shape=(jax....]
where the time goes in v2:
time: 849 us
  Pallas kernels  838 us (99%)
  local copies, waits for them, and re-layouts  9.88 us (1%)
    pallas_call x1, Pallas kernels, local_steps(): pl.pallas_call(functools.partial(lanczos_kernel, ts, nd), out_shape=(jax....  838 us

profile of v2, /device:TPU:0, one launch (start us, length us, event | category | flops | bytes accessed | tf_op | source)
XLA Modules:
  0.0 849.0 jit_solution(5062531032592065431)
XLA Ops:
  0.6 1.1 copy.8
  1.7 0.7 reshape.19.w2
  2.5 2.9 reshape.18.psi
  5.4 838.5 %shard_map.67 = (f32[512,512]{1,0:T(8,128)}, f32[4]{0:T(128)}, f32[4]{0:T(128)}) custom-call(f32[512,512]{1,0:T(8,128)} %reshape.18.psi, f32[28,28]{1,0:T(8,128)} %reshape.19.w2, f32[14,256,2048]{2,1,0:T(8,128)} %bitcast.6, f32[56,128,2048]{2,1,0:T(8,128)} %bitcast.5), custom_call_target="tpu_custom_call" | custom-call | tf_op jit(solution)/shard_map/pallas_call | solution.py:474
  843.9 2.8 reshape.21
  846.7 1.1 copy.11
  847.8 1.2 copy.12

commit v3 on v2

--- a/solution.py
+++ b/solution.py
@@ -31,9 +31,9 @@
     return hi, mid, low
 
 
-def lanczos_kernel(ts, nd, psi, w2, lt, rt, out_v, out_a, out_b,
-                   psi_v, vy, vcur, vprev, wprime, recv, t1, t2, l0, l1, r0, r1, vp, wk6, ar_src, ar_recv,
-                   lsem, rsem, vsend, vrecv, ysend, yrecv, asend, arecv, iosem, fwd_ok, back_ok):
+def lanczos_kernel(ts, nd, psi, w_in, lt, rt, out_v, out_ab,
+                   psi_v, wv, norms, vy, vcur, vprev, wprime, recv, t1, t2, l0, l1, r0, r1, vp, wk6, ar_src, ar_recv,
+                   lsem, rsem, vsend, vrecv, ysend, yrecv, asend, arecv, iosem, wsem, fwd_ok, back_ok):
     row, col = lax.axis_index("row"), lax.axis_index("col")
     me = col * NROW + row
     core, xx, yy = mod(row, 2), mod(div(row, 2), 2), div(row, 4)
@@ -64,13 +64,13 @@
         h_in = (1 - late) * two + late * odd
         return (1 - mz) * (3 - two) + mz * d_in, (1 - mz) * odd + mz * h_in
 
-    def l_batch(g):
-        slot = mod(g, 2)
-        a0 = pl.multiple_of(row_of(g) * ts, ts)
-        a1 = pl.multiple_of(row_of(mod(g + 1, 8)) * ts, ts)
-        pltpu.make_async_copy(lt.at[pl.ds(1, nd - 1), :, pl.ds(a0, ts)],
+    def l_start(g):
+        return pl.multiple_of(row_of(mod(g, 8)) * ts, ts)
+
+    def l_batch(slot, a0, a1):
+        pltpu.make_async_copy(lt.at[pl.ds(1, nd - 1), :, pl.ds(pl.multiple_of(a0, ts), ts)],
                               recv.at[pl.ds(nd * slot, nd - 1)], lsem.at[slot]).start()
-        pltpu.make_async_copy(lt.at[pl.ds(0, 1), :, pl.ds(a1, ts)],
+        pltpu.make_async_copy(lt.at[pl.ds(0, 1), :, pl.ds(pl.multiple_of(a1, ts), ts)],
                               recv.at[pl.ds(nd * slot + nd - 1, 1)], lsem.at[slot]).start()
 
     def l_batch_wait(slot):
@@ -78,7 +78,7 @@
         pltpu.make_async_copy(ref, ref, lsem.at[slot]).wait()
 
     def r_start(i):
-        dm, h = block_of(i)
+        dm, h = block_of(mod(i, 8))
         dest = dm + half_z * (3 - 2 * dm)
         return pl.multiple_of((dest * 2 + h) * ts, ts)
 
@@ -87,12 +87,10 @@
 
     half = nd // 2
 
-    def r_batch(i):
-        slot = mod(i, 2)
-        d0, d1 = r_start(i), r_start(mod(i + 1, 8))
+    def r_batch(slot, d0, d1):
         for first, count, d, hh, plane in ((1, half, d0, 0, 0), (half + 1, half - 1, d0, 1, 0), (0, 1, d1, 1, 4 * half - 4)):
             if count:
-                pltpu.make_async_copy(rt.at[pl.ds(4 * first, 4 * count), :, pl.ds(d, ts)],
+                pltpu.make_async_copy(rt.at[pl.ds(4 * first, 4 * count), :, pl.ds(pl.multiple_of(d, ts), ts)],
                                       t1.at[pl.ds(plane, 4 * count), r_rows(slot), pl.ds(hh * ts, ts)],
                                       rsem.at[slot]).start()
 
@@ -168,23 +166,38 @@
         return jnp.where(first, jnp.broadcast_to(a, (2, 128)), jnp.broadcast_to(b, (2, 128)))
 
     def vec(x):
-        return jnp.full((8, 128), x, F32)
-
-    def scaled_start(src_norm_coef):
-        def scale(i, sq):
+        return jnp.full((8, W8), x, F32)
+
+    def times(x, v):
+        wide = v if x.shape[-1] == v.shape[-1] else jnp.concatenate([v] * (x.shape[-1] // v.shape[-1]), axis=1)
+        return (x.reshape(-1, 8, x.shape[-1]) * wide[None]).reshape(x.shape)
+
+    def first_start(scale):
+        def part(i, sq):
             n, rows = where_is(i)
             x = wprime[n, rows, :]
-            vy[0, n, rows, :] = x * src_norm_coef
+            vy[0, n, rows, :] = times(x, scale)
             return sq + fold(jnp.add, x * x)
 
-        sq = lax.fori_loop(0, nblk, scale, jnp.zeros((8, W8), F32))
+        sq = lax.fori_loop(0, nblk, part, jnp.zeros((8, W8), F32))
         ar_start(1, two_rows(as_row(sq, jnp.sum), jnp.zeros((1, 128), F32)))
 
+    barrier = pltpu.get_barrier_semaphore()
+
+    def arrive(off, carry):
+        to = mod(me + off, NDEV)
+        pl.semaphore_signal(barrier, inc=1, device_id={"col": div(to, NROW), "row": mod(to, NROW)},
+                            device_id_type=pl.DeviceIdType.MESH)
+        return carry
+
+    lax.fori_loop(1, NDEV, arrive, 0)
     LB = min(128, ts)
     blocks = range(2 * ts // LB)
-    loads = [pltpu.make_async_copy(psi.at[:, pl.ds(b * LB, LB)], psi_v.at[b], iosem.at[b]) for b in blocks]
+    loads = [pltpu.make_async_copy(psi.at[:, :, pl.ds(b * LB, LB)], psi_v.at[b].reshape(ts, 2, LB), iosem.at[b]) for b in blocks]
     for load in loads:
         load.start()
+    w_load = pltpu.make_async_copy(w_in, wv, wsem)
+    w_load.start()
     l_first = pltpu.make_async_copy(lt.at[pl.ds(0, 1), :, pl.ds(pl.multiple_of(row * ts, ts), ts)],
                                     recv.at[pl.ds(2 * nd - 1, 1)], lsem.at[1])
     l_first.start()
@@ -192,7 +205,7 @@
     r_first = pltpu.make_async_copy(rt.at[pl.ds(0, 4), :, pl.ds(r_start(zero_i), ts)],
                                     t1.at[pl.ds(4 * half - 4, 4), r_rows(1), pl.ds(ts, ts)], rsem.at[1])
     r_first.start()
-    l_batch(zero_i)
+    l_batch(zero_i, l_start(zero_i), l_start(zero_i + 1))
     for b, load in enumerate(loads):
         load.wait()
         for sp in range(2):
@@ -205,10 +218,13 @@
         return jnp.maximum(mx, fold(jnp.maximum, jnp.abs(x)))
 
     mx = lax.fori_loop(0, nblk, biggest, jnp.zeros((8, W8), F32))
+    pl.semaphore_wait(barrier, NDEV - 1)
     ar_start(0, two_rows(jnp.zeros((1, 128), F32), as_row(mx, jnp.max)))
-    pieces = split3(w2[...])
-    up = (div(lax.broadcasted_iota(jnp.int32, (kron, 2 * nd), 0), KRON)
-          == lax.broadcasted_iota(jnp.int32, (kron, 2 * nd), 1)).astype(F32).astype(BF16)
+    w_load.wait()
+    pieces = [split3(wv[:, t, :]) for t in range(2)]
+    at_row = lax.broadcasted_iota(jnp.int32, (kron, nd), 0)
+    up = [((div(at_row, 2 * KRON) == lax.broadcasted_iota(jnp.int32, (kron, nd), 1)) & (mod(div(at_row, KRON), 2) == t))
+          .astype(F32).astype(BF16) for t in range(2)]
     lane = lax.broadcasted_iota(jnp.int32, (2 * nd, 6 * kron), 1)
     across = (div(mod(lane, kron), KRON) == lax.broadcasted_iota(jnp.int32, (2 * nd, 6 * kron), 0)).astype(F32).astype(BF16)
     lane = lax.broadcasted_iota(jnp.int32, (kron, 6 * kron), 1)
@@ -216,7 +232,8 @@
     which = div(lane, kron)
     total = jnp.zeros((kron, 6 * kron), F32)
     for k in range(3):
-        tall = jnp.dot(up, pieces[k], preferred_element_type=F32).astype(BF16)
+        tall = sum(lax.dot_general(up[t], pieces[t][k], (((1,), (1,)), ((), ())), preferred_element_type=F32)
+                   for t in range(2)).astype(BF16)
         wide = jnp.dot(tall, across, preferred_element_type=F32)
         here = [n for n, kk in enumerate(kk for p, n2 in PASSES for kk in range(n2)) if kk == k]
         mask = same & functools.reduce(jnp.logical_or, [which == n for n in here])
@@ -227,12 +244,14 @@
     r_first.wait()
     r_split(1, nd - 1, r0)
     _, gmax = ar_wait(0)
-    scaled_start(jnp.max(1.0 / vec(gmax)) * (2.0 ** -12))
+    first_start((1.0 / vec(gmax)) * (2.0 ** -12))
+
+    peers = {s: row_of(jnp.int32(s)) for s in (0, 1, 2, 4, 6)}
 
     def v_copy(src, slot, s):
         return pltpu.make_async_remote_copy(
             src_ref=vy.at[src], dst_ref=vy.at[slot], send_sem=vsend.at[slot], recv_sem=vrecv.at[slot],
-            device_id={"row": row_of(s)}, device_id_type=pl.DeviceIdType.MESH)
+            device_id={"row": peers[s]}, device_id_type=pl.DeviceIdType.MESH)
 
     def swap(a, b):
         a, b = a.reshape(-1, 8, a.shape[-1]), b.reshape(-1, 8, b.shape[-1])
@@ -248,6 +267,8 @@
                 t1[at] = jnp.where(keep, t1[at], 0.0) + both[e].reshape(ts, ts)
 
     def t1_group(g, carry):
+        slot, a1, a2 = carry
+
         @pl.when(g > 0)
         def _():
             v_copy(0, g, 0).wait_recv()
@@ -256,15 +277,15 @@
         def _():
             v_copy(g, g + 1, 1).start()
 
-        @pl.when((g == 1) | (g == 2))
-        def _():
-            v_copy(0, 2 + 2 * g, 2 + 2 * g).start()
+        for first, s in ((1, 4), (2, 6)):
+            @pl.when(g == first)
+            def _():
+                v_copy(0, s, s).start()
 
         @pl.when(g < 7)
         def _():
-            l_batch(g + 1)
-
-        slot = mod(g, 2)
+            l_batch(1 - slot, a1, a2)
+
         l_batch_wait(slot)
         for n in range(4):
             for b in range(ts // SB):
@@ -274,26 +295,28 @@
         for k in range(nd):
             l_split(slot, k, lps[(k + 1) % 2])
             t1_chunk(lps[k % 2], k, g > 0)
-        return carry
+        return 1 - slot, a2, l_start(g + 3)
 
     t2_rows = min(64, hs)
 
     def t2_trip(i, carry):
         @pl.when(i == (hs // t2_rows))
         def _():
-            r_batch(zero_i)
+            r_batch(zero_i, r_start(zero_i), r_start(zero_i + 1))
 
         c0 = pl.multiple_of(i * t2_rows, t2_rows)
         for h in range(t2_rows // 8):
-            x = t1[:, pl.ds(c0 + h * 8, 8), :].reshape(nd, 2, 8, 2 * ts)
-            parts = []
-            for e in range(2):
-                b = split3(x[:, e].reshape(kron, 2 * ts))
-                rhs = jnp.concatenate([b[p] for p, n in PASSES for _ in range(n)], axis=0)
-                got = jnp.dot(wk6[...], rhs, preferred_element_type=F32)
-                parts.append(got.reshape(nd, 8, 2 * ts))
-            for p, y in enumerate(split3(jnp.concatenate(parts, axis=1))):
-                t2[p, :, pl.ds(2 * c0 + h * 16, 16), :] = y
+            for q in range(2):
+                cols = pl.ds(q * ts, ts)
+                x = t1[:, pl.ds(c0 + h * 8, 8), cols].reshape(nd, 2, 8, ts)
+                parts = []
+                for e in range(2):
+                    b = split3(x[:, e].reshape(kron, ts))
+                    rhs = jnp.concatenate([b[p] for p, n in PASSES for _ in range(n)], axis=0)
+                    got = jnp.dot(wk6[...], rhs, preferred_element_type=F32)
+                    parts.append(got.reshape(nd, 8, ts))
+                for p, y in enumerate(split3(jnp.concatenate(parts, axis=1))):
+                    t2[p, :, pl.ds(2 * c0 + h * 16, 16), cols] = y
         return carry
 
     def y_copy(src, idx, slot, to):
@@ -322,20 +345,20 @@
                    [pieces[k].reshape(2 * ts, ts) for k in range(3)])
 
     def t3_part(factor, i, carry):
+        slot, d1, d2 = carry
         dm, h = block_of(i)
 
         @pl.when(i < 7)
         def _():
-            r_batch(i + 1)
-
-        slot = mod(i, 2)
+            r_batch(1 - slot, d1, d2)
+
         r_batch_wait(slot)
         total = None
         for k in range(nd):
             r_split(slot, k, rps[(k + 1) % 2])
             got = t3_chunk(rps[k % 2], k)
             total = got if total is None else total + got
-        total = (total * factor).reshape(ts // 8, 16, ts)
+        total = times(total, factor).reshape(ts // 8, 16, ts)
         for e, y in enumerate(swap(total[:, :8], total[:, 8:])):
             vy[4 + dm, 2 * h + e] = y.reshape(ts, ts)
 
@@ -363,13 +386,13 @@
             add_into(0, k, 6 + k)
             y_copy(y_ref(0, k), k, 6 + k, col - zdir).start()
 
-        return carry
+        return 1 - slot, d2, r_start(i + 3)
 
     def step(j, state):
-        gmax, beta_prev = state
+        gmax = state
         for s in (1, 2):
             v_copy(0, s, s).start()
-        lax.fori_loop(0, 8, t1_group, 0)
+        lax.fori_loop(0, 8, t1_group, (zero_i, l_start(zero_i + 1), l_start(zero_i + 2)))
         for s in range(1, 8):
             v_copy(0, s, 0).wait_send()
 
@@ -384,44 +407,36 @@
 
         total, _ = ar_wait(1)
         norm_v = jnp.sqrt(vec(total))
-        norm = jnp.max(norm_v)
-        inv = jnp.max(1.0 / norm_v)
-        factor = jnp.max(vec(gmax) / norm_v) * (2.0 ** 12)
-        beta_prev = jnp.where(j > 0, norm, 0.0)
-
-        @pl.when(j > 0)
-        def _():
-            out_b[j - 1] = norm
+        inv = 1.0 / norm_v
+        factor = vec(gmax) * inv * (2.0 ** 12)
+        beta_prev = jnp.where(j > 0, norm_v, 0.0)
+        norms[j] = norm_v
 
         lax.fori_loop(0, ts // t2_rows, t2_trip, 0)
-        lax.fori_loop(0, 8, functools.partial(t3_part, factor), 0)
+        lax.fori_loop(0, 8, functools.partial(t3_part, factor), (zero_i, r_start(zero_i + 1), r_start(zero_i + 2)))
+
+        own = 4 + mz
+        near = 6 - 2 * mz
+        for h in range(2):
+            y_copy(landing(0), 0, near + h, col).wait_recv()
 
         @pl.when(mz == 0)
         def _():
-            for h in range(2):
-                add_into(0, h, 6 + h)
             for k in range(6):
                 y_copy(y_ref(0, 0), k, k, col).wait_send()
 
         @pl.when(mz == 1)
         def _():
             for h in range(2):
-                add_into(1, h, 4 + h)
-                add_into(1, h, 8 + h)
+                y_copy(landing(0), 0, 8 + h, col).wait_recv()
             for k in (0, 1, 6, 7, 8, 9):
                 y_copy(y_ref(0, 0), k, k, col).wait_send()
-
-        own = 4 + mz
-
-        @pl.when(j < STEPS - 1)
-        def _():
-            l_batch(zero_i)
 
         def dots(i, c):
             n, rows = where_is(i)
             dot, mx = c
-            w = vy[own, n, rows, :]
-            v = wprime[n, rows, :] * inv
+            w = vy[own, n, rows, :] + recv[2 * near + n, rows, :] + jnp.where(mz == 1, recv[16 + n, rows, :], 0.0)
+            v = times(wprime[n, rows, :], inv)
             vcur[n, rows, :] = v
             wprime[n, rows, :] = w
             return dot + fold(jnp.add, v * w), jnp.maximum(mx, fold(jnp.maximum, jnp.abs(w)))
@@ -429,65 +444,71 @@
         zero = jnp.zeros((8, W8), F32)
         dot, mx = lax.fori_loop(0, nblk, dots, (zero, zero))
         ar_start(0, two_rows(as_row(dot, jnp.sum), as_row(mx, jnp.max)))
+
+        @pl.when(j < STEPS - 1)
+        def _():
+            l_batch(zero_i, l_start(zero_i), l_start(zero_i + 1))
+
         alpha, gmax = ar_wait(0)
-        out_a[j] = alpha
-        small = jnp.max(1.0 / vec(gmax)) * (2.0 ** -12)
+        out_ab[j] = alpha
+        small = (1.0 / vec(gmax)) * (2.0 ** -12)
 
         def update(i, sq):
             n, rows = where_is(i)
             v = vcur[n, rows, :]
-            x = wprime[n, rows, :] - alpha * v - beta_prev * vprev[n, rows, :]
+            x = wprime[n, rows, :] - alpha * v - times(vprev[n, rows, :], beta_prev)
             vprev[n, rows, :] = v
             wprime[n, rows, :] = x
-            vy[0, n, rows, :] = x * small
+            vy[0, n, rows, :] = times(x, small)
             return sq + fold(jnp.add, x * x)
 
         sq = lax.fori_loop(0, nblk, update, zero)
         ar_start(1, two_rows(as_row(sq, jnp.sum), jnp.zeros((1, 128), F32)))
-        return gmax, norm
-
-    lax.fori_loop(0, STEPS, step, (gmax, jnp.float32(0)))
+        return gmax
+
+    lax.fori_loop(0, STEPS, step, gmax)
 
     total, _ = ar_wait(1)
     norm_v = jnp.sqrt(vec(total))
-    inv = jnp.max(1.0 / norm_v)
-    out_b[STEPS - 1] = jnp.max(norm_v)
-
-    stores = [pltpu.make_async_copy(psi_v.at[b], out_v.at[:, pl.ds(b * LB, LB)], iosem.at[b]) for b in blocks]
+    inv = 1.0 / norm_v
+    norms[STEPS] = norm_v
+    stores = [pltpu.make_async_copy(psi_v.at[b].reshape(ts, 2, LB), out_v.at[:, :, pl.ds(b * LB, LB)], iosem.at[b]) for b in blocks]
     for b, store in enumerate(stores):
         for sp in range(2):
-            psi_v[b, pl.ds(sp, ts, stride=2), :] = wprime[2 * (b * LB // ts) + sp, :, pl.ds(b * LB % ts, LB)] * inv
+            psi_v[b, pl.ds(sp, ts, stride=2), :] = times(
+                wprime[2 * (b * LB // ts) + sp, :, pl.ds(b * LB % ts, LB)], inv)
         store.start()
+    for j in range(STEPS):
+        out_ab[STEPS + j] = jnp.max(norms[j + 1])
     for store in stores:
         store.wait()
 
 
 def local_steps(ts, nd, psi_blk, left_blk, mpo_tensor, right_blk):
-    psi = psi_blk.reshape(2 * ts, 2 * ts)
     lt = left_blk.transpose(1, 0, 2)
     rt = right_blk.transpose(1, 0, 2).reshape(4 * nd, ts // 2, 8 * ts)
-    w2 = mpo_tensor.transpose(1, 3, 0, 2).reshape(2 * nd, 2 * nd)
+    w_in = mpo_tensor.transpose(0, 2, 3, 1).reshape(2 * nd, 2, nd)
     any_space = pl.BlockSpec(memory_space=pl.ANY)
-    vmem = pl.BlockSpec(memory_space=pltpu.VMEM)
     dma, V = pltpu.SemaphoreType.DMA, pltpu.VMEM
     smem = pl.BlockSpec(memory_space=pltpu.SMEM)
-    out_v, alpha, beta = pl.pallas_call(
+    out_v, out_ab = pl.pallas_call(
         functools.partial(lanczos_kernel, ts, nd),
-        out_shape=(jax.ShapeDtypeStruct((2 * ts, 2 * ts), F32),) + (jax.ShapeDtypeStruct((STEPS,), F32),) * 2,
-        in_specs=[any_space, vmem, any_space, any_space],
-        out_specs=(any_space, smem, smem),
+        out_shape=(jax.ShapeDtypeStruct((ts, 2, 2 * ts), F32), jax.ShapeDtypeStruct((2 * STEPS,), F32)),
+        in_specs=[any_space] * 4,
+        out_specs=(any_space, smem),
         scratch_shapes=[
-            V((2 * ts // min(128, ts), 2 * ts, min(128, ts)), F32), V((8, 4, ts, ts), F32), V((4, ts, ts), F32), V((4, ts, ts), F32), V((4, ts, ts), F32),
+            V((2 * ts // min(128, ts), 2 * ts, min(128, ts)), F32), V((2 * nd, 2, nd), F32), V((STEPS + 1, 8, min(128, ts)), F32),
+            V((8, 4, ts, ts), F32), V((4, ts, ts), F32), V((4, ts, ts), F32), V((4, ts, ts), F32),
             V((max(20, 2 * nd), ts, ts), F32), V((2 * nd, ts, 2 * ts), F32), V((3, nd, 2 * ts, 2 * ts), BF16),
             V((3, ts, ts), BF16), V((3, ts, ts), BF16), V((3, 2, ts, ts), BF16), V((3, 2, ts, ts), BF16),
             V((3, ts, 4 * ts), BF16), V((2 * nd * KRON, 12 * nd * KRON), BF16),
             V((2, 2, 128), F32), V((2, NDEV, 2, 128), F32),
-            dma((2,)), dma((2,)), dma((8,)), dma((8,)), dma((10,)), dma((10,)), dma((2,)), dma((2,)), dma((4,)),
+            dma((2,)), dma((2,)), dma((8,)), dma((8,)), dma((10,)), dma((10,)), dma((2,)), dma((2,)), dma((4,)), dma,
             pltpu.SemaphoreType.REGULAR, pltpu.SemaphoreType.REGULAR,
         ],
-        compiler_params=pltpu.CompilerParams(vmem_limit_bytes=67043328, has_side_effects=True),
-    )(psi, w2, lt, rt)
-    return alpha, beta, out_v.reshape(ts, 2, 2 * ts)
+        compiler_params=pltpu.CompilerParams(vmem_limit_bytes=67043328, has_side_effects=True, collective_id=0),
+    )(psi_blk, w_in, lt, rt)
+    return out_ab[:STEPS], out_ab[STEPS:], out_v
 
 
 def build(mesh, ts, nd):

time: 849 us -> 823 us (0.969)
  Pallas kernels: 838 us -> 818 us
    pallas_call x1, Pallas kernels: 838 us -> 818 us  [local_steps(): pl.pallas_call(functools.partial(lanczos_kernel, ts, nd), out_shape=(jax....]
where the time goes in v3:
time: 823 us
  Pallas kernels  818 us (99%)
    pallas_call x1, Pallas kernels, local_steps(): pl.pallas_call(functools.partial(lanczos_kernel, ts, nd), out_shape=(jax....  818 us

profile of v3, /device:TPU:0, one launch (start us, length us, event | category | flops | bytes accessed | tf_op | source)
XLA Modules:
  0.0 823.0 jit_solution(11942019547930760803)
XLA Ops:
  0.6 818.5 %shard_map.67 = (f32[256,2,512]{2,1,0:T(2,128)}, f32[8]{0:T(128)}) custom-call(f32[256,2,512]{2,1,0:T(2,128)} %psi.1, f32[28,2,14]{2,1,0:T(2,128)} %bitcast.9, f32[14,256,2048]{2,1,0:T(8,128)} %bitcast.8, f32[56,128,2048]{2,1,0:T(8,128)} %bitcast.7), custom_call_target="tpu_custom_call" | custom-call | tf_op jit(solution)/shard_map/pallas_call | solution.py:494
  819.1 1.3 fusion
  820.4 2.6 copy.8

commit v4 on v3

--- a/solution.py
+++ b/solution.py
@@ -31,8 +31,8 @@
     return hi, mid, low
 
 
-def lanczos_kernel(ts, nd, psi, w_in, lt, rt, out_v, out_ab,
-                   psi_v, wv, norms, vy, vcur, vprev, wprime, recv, t1, t2, l0, l1, r0, r1, vp, wk6, ar_src, ar_recv,
+def lanczos_kernel(ts, nd, psi, w_in, lt, rt, out_w, out_s,
+                   psi_v, wv, norms, mults, vy, vcur, vprev, wprime, recv, t1, t2, l0, l1, r0, r1, vp, wk_a, wk_b, ar_src, ar_recv,
                    lsem, rsem, vsend, vrecv, ysend, yrecv, asend, arecv, iosem, wsem, fwd_ok, back_ok):
     row, col = lax.axis_index("row"), lax.axis_index("col")
     me = col * NROW + row
@@ -136,10 +136,15 @@
             device_id={"col": col, "row": row}, device_id_type=pl.DeviceIdType.MESH)
         copy.wait_send()
         copy.wait_recv()
+
+    def ar_read(slot):
         got = ar_recv[slot]
-        first = lax.broadcasted_iota(jnp.int32, got.shape, 1) == 0
-        return jnp.sum(jnp.where(first, got, 0.0)), jnp.max(jnp.where(first, 0.0, got))
-
+        total, most = jnp.sum(got, axis=0), jnp.max(got, axis=0)
+        total = jnp.sum(total[0:1], axis=1, keepdims=True)
+        most = jnp.max(most[1:2], axis=1, keepdims=True)
+        return jnp.broadcast_to(total, (8, W8)), jnp.broadcast_to(most, (8, W8))
+
+    W8 = min(128, ts)
     RB = min(64, ts)
     nblk = 4 * (ts // RB)
 
@@ -147,16 +152,14 @@
         return div(i, ts // RB), pl.ds(pl.multiple_of(mod(i, ts // RB) * RB, RB), RB)
 
     def fold(op, x):
-        x = x.reshape(RB // 8, 8, ts)
+        x = x.reshape(-1, 8, ts)
         y = x[0]
-        for k in range(1, RB // 8):
+        for k in range(1, x.shape[0]):
             y = op(y, x[k])
         if ts <= 128:
             return y
         return op(y[:, :128], y[:, 128:])
 
-    W8 = min(128, ts)
-
     def as_row(x, op):
         x = op(x, axis=0, keepdims=True)
         return x if W8 == 128 else jnp.concatenate([x, jnp.zeros((1, 128 - W8), F32)], axis=1)
@@ -164,9 +167,6 @@
     def two_rows(a, b):
         first = lax.broadcasted_iota(jnp.int32, (2, 128), 0) == 0
         return jnp.where(first, jnp.broadcast_to(a, (2, 128)), jnp.broadcast_to(b, (2, 128)))
-
-    def vec(x):
-        return jnp.full((8, W8), x, F32)
 
     def times(x, v):
         wide = v if x.shape[-1] == v.shape[-1] else jnp.concatenate([v] * (x.shape[-1] // v.shape[-1]), axis=1)
@@ -225,26 +225,26 @@
     at_row = lax.broadcasted_iota(jnp.int32, (kron, nd), 0)
     up = [((div(at_row, 2 * KRON) == lax.broadcasted_iota(jnp.int32, (kron, nd), 1)) & (mod(div(at_row, KRON), 2) == t))
           .astype(F32).astype(BF16) for t in range(2)]
-    lane = lax.broadcasted_iota(jnp.int32, (2 * nd, 6 * kron), 1)
-    across = (div(mod(lane, kron), KRON) == lax.broadcasted_iota(jnp.int32, (2 * nd, 6 * kron), 0)).astype(F32).astype(BF16)
-    lane = lax.broadcasted_iota(jnp.int32, (kron, 6 * kron), 1)
-    same = mod(lane, KRON) == mod(lax.broadcasted_iota(jnp.int32, (kron, 6 * kron), 0), KRON)
-    which = div(lane, kron)
-    total = jnp.zeros((kron, 6 * kron), F32)
+    lane = lax.broadcasted_iota(jnp.int32, (2 * nd, 256), 1)
+    across = ((div(mod(lane, kron), KRON) == lax.broadcasted_iota(jnp.int32, (2 * nd, 256), 0)) & (lane < 2 * kron))
+    across = across.astype(F32).astype(BF16)
+    lane = lax.broadcasted_iota(jnp.int32, (kron, 256), 1)
+    same = mod(lane, KRON) == mod(lax.broadcasted_iota(jnp.int32, (kron, 256), 0), KRON)
+    wide = []
     for k in range(3):
         tall = sum(lax.dot_general(up[t], pieces[t][k], (((1,), (1,)), ((), ())), preferred_element_type=F32)
                    for t in range(2)).astype(BF16)
-        wide = jnp.dot(tall, across, preferred_element_type=F32)
-        here = [n for n, kk in enumerate(kk for p, n2 in PASSES for kk in range(n2)) if kk == k]
-        mask = same & functools.reduce(jnp.logical_or, [which == n for n in here])
-        total = jnp.where(mask, wide, total)
-    wk6[...] = total.astype(BF16)
+        wide.append(jnp.where(same, jnp.dot(tall, across, preferred_element_type=F32), 0.0))
+    for k in range(2):
+        wk_a[pl.ds(k * kron, kron), :] = wide[k].astype(BF16)
+    wk_b[...] = jnp.where(lane < kron, wide[2], wide[0]).astype(BF16)
     l_first.wait()
     l_split(1, nd - 1, l0)
     r_first.wait()
     r_split(1, nd - 1, r0)
-    _, gmax = ar_wait(0)
-    first_start((1.0 / vec(gmax)) * (2.0 ** -12))
+    ar_wait(0)
+    _, gmax = ar_read(0)
+    first_start((1.0 / gmax) * (2.0 ** -12))
 
     peers = {s: row_of(jnp.int32(s)) for s in (0, 1, 2, 4, 6)}
 
@@ -297,13 +297,18 @@
             t1_chunk(lps[k % 2], k, g > 0)
         return 1 - slot, a2, l_start(g + 3)
 
-    t2_rows = min(64, hs)
-
-    def t2_trip(i, carry):
+    t2_rows = min(128, hs)
+
+    def t2_trip(j, gmax, i, carry):
         @pl.when(i == (hs // t2_rows))
         def _():
             r_batch(zero_i, r_start(zero_i), r_start(zero_i + 1))
 
+        norm = jnp.sqrt(ar_read(1)[0])
+        inv = 1.0 / norm
+        norms[j] = norm
+        mults[0] = inv
+        mults[1] = gmax * inv * (2.0 ** 12)
         c0 = pl.multiple_of(i * t2_rows, t2_rows)
         for h in range(t2_rows // 8):
             for q in range(2):
@@ -312,9 +317,10 @@
                 parts = []
                 for e in range(2):
                     b = split3(x[:, e].reshape(kron, ts))
-                    rhs = jnp.concatenate([b[p] for p, n in PASSES for _ in range(n)], axis=0)
-                    got = jnp.dot(wk6[...], rhs, preferred_element_type=F32)
-                    parts.append(got.reshape(nd, 8, ts))
+                    low = jnp.zeros((256 - 2 * kron, ts), BF16)
+                    first = jnp.dot(wk_a[...], jnp.concatenate([b[0], b[1], low], axis=0), preferred_element_type=F32)
+                    last = jnp.dot(wk_b[...], jnp.concatenate([b[0], b[2], low], axis=0), preferred_element_type=F32)
+                    parts.append((first[:kron] + first[kron:] + last).reshape(nd, 8, ts))
                 for p, y in enumerate(split3(jnp.concatenate(parts, axis=1))):
                     t2[p, :, pl.ds(2 * c0 + h * 16, 16), cols] = y
         return carry
@@ -333,18 +339,10 @@
     def add_into(dm, h, slot):
         y_copy(landing(slot), 0, slot, col).wait_recv()
 
-        def add(i, c):
-            n, rows = where_is(i)
-            vy[4 + dm, 2 * h + n, rows, :] = vy[4 + dm, 2 * h + n, rows, :] + recv[2 * slot + n, rows, :]
-            return c
-
-        lax.fori_loop(0, nblk // 2, add, 0)
-
-    def t3_chunk(pieces, r):
-        return six([t2[k, r] for k in range(3)],
-                   [pieces[k].reshape(2 * ts, ts) for k in range(3)])
-
-    def t3_part(factor, i, carry):
+        for n in range(2):
+            vy[4 + dm, 2 * h + n] = vy[4 + dm, 2 * h + n] + recv[2 * slot + n]
+
+    def t3_part(i, carry):
         slot, d1, d2 = carry
         dm, h = block_of(i)
 
@@ -353,14 +351,17 @@
             r_batch(1 - slot, d1, d2)
 
         r_batch_wait(slot)
-        total = None
+        total = [None, None]
         for k in range(nd):
             r_split(slot, k, rps[(k + 1) % 2])
-            got = t3_chunk(rps[k % 2], k)
-            total = got if total is None else total + got
-        total = times(total, factor).reshape(ts // 8, 16, ts)
-        for e, y in enumerate(swap(total[:, :8], total[:, 8:])):
-            vy[4 + dm, 2 * h + e] = y.reshape(ts, ts)
+            if k == 1:
+                d3 = r_start(i + 3)
+            for q in range(2):
+                got = six([t2[p, k, pl.ds(q * ts, ts)] for p in range(3)],
+                          [rps[k % 2][p].reshape(2 * ts, ts) for p in range(3)])
+                total[q] = got if total[q] is None else total[q] + got
+        for q in range(2):
+            vy[4 + dm, 2 * h + q] = total[q]
 
         @pl.when(i == 2 * mz)
         def _():
@@ -386,7 +387,7 @@
             add_into(0, k, 6 + k)
             y_copy(y_ref(0, k), k, 6 + k, col - zdir).start()
 
-        return 1 - slot, d2, r_start(i + 3)
+        return 1 - slot, d2, d3
 
     def step(j, state):
         gmax = state
@@ -405,15 +406,9 @@
             pl.semaphore_signal(fwd_ok, inc=1, device_id={"col": col + zdir}, device_id_type=pl.DeviceIdType.MESH)
             pl.semaphore_signal(fwd_ok, inc=1, device_id={"col": col - zdir}, device_id_type=pl.DeviceIdType.MESH)
 
-        total, _ = ar_wait(1)
-        norm_v = jnp.sqrt(vec(total))
-        inv = 1.0 / norm_v
-        factor = vec(gmax) * inv * (2.0 ** 12)
-        beta_prev = jnp.where(j > 0, norm_v, 0.0)
-        norms[j] = norm_v
-
-        lax.fori_loop(0, ts // t2_rows, t2_trip, 0)
-        lax.fori_loop(0, 8, functools.partial(t3_part, factor), (zero_i, r_start(zero_i + 1), r_start(zero_i + 2)))
+        ar_wait(1)
+        lax.fori_loop(0, ts // t2_rows, functools.partial(t2_trip, j, gmax), 0)
+        lax.fori_loop(0, 8, t3_part, (zero_i, r_start(zero_i + 1), r_start(zero_i + 2)))
 
         own = 4 + mz
         near = 6 - 2 * mz
@@ -432,31 +427,43 @@
             for k in (0, 1, 6, 7, 8, 9):
                 y_copy(y_ref(0, 0), k, k, col).wait_send()
 
+        inv, factor = mults[0], mults[1]
+        CB = min(32, hs)
+
         def dots(i, c):
-            n, rows = where_is(i)
             dot, mx = c
-            w = vy[own, n, rows, :] + recv[2 * near + n, rows, :] + jnp.where(mz == 1, recv[16 + n, rows, :], 0.0)
-            v = times(wprime[n, rows, :], inv)
-            vcur[n, rows, :] = v
-            wprime[n, rows, :] = w
-            return dot + fold(jnp.add, v * w), jnp.maximum(mx, fold(jnp.maximum, jnp.abs(w)))
+            h, b = div(i, ts // CB), mod(i, ts // CB)
+            n, rows = div(b, ts // (2 * CB)), pl.ds(pl.multiple_of(mod(b, ts // (2 * CB)) * 2 * CB, 2 * CB), 2 * CB)
+            n = 2 * h + n
+            y = vy[own, n, rows, :] + recv[2 * near + n, rows, :] + jnp.where(mz == 1, recv[16 + n, rows, :], 0.0)
+            y = times(y, factor).reshape(CB // 8, 16, ts)
+            at = pl.ds(pl.multiple_of(b * CB, CB), CB)
+            for t, w in enumerate(swap(y[:, :8], y[:, 8:])):
+                w = w.reshape(CB, ts)
+                v = times(wprime[2 * h + t, at, :], inv)
+                vcur[2 * h + t, at, :] = v
+                wprime[2 * h + t, at, :] = w
+                dot, mx = dot + fold(jnp.add, v * w), jnp.maximum(mx, fold(jnp.maximum, jnp.abs(w)))
+            return dot, mx
 
         zero = jnp.zeros((8, W8), F32)
-        dot, mx = lax.fori_loop(0, nblk, dots, (zero, zero))
+        dot, mx = lax.fori_loop(0, 2 * (ts // CB), dots, (zero, zero))
         ar_start(0, two_rows(as_row(dot, jnp.sum), as_row(mx, jnp.max)))
 
         @pl.when(j < STEPS - 1)
         def _():
             l_batch(zero_i, l_start(zero_i), l_start(zero_i + 1))
 
-        alpha, gmax = ar_wait(0)
-        out_ab[j] = alpha
-        small = (1.0 / vec(gmax)) * (2.0 ** -12)
+        ar_wait(0)
+        alpha, gmax = ar_read(0)
+        out_s[j] = alpha
+        small = (1.0 / gmax) * (2.0 ** -12)
+        beta_prev = jnp.where(j > 0, norms[j], 0.0)
 
         def update(i, sq):
             n, rows = where_is(i)
             v = vcur[n, rows, :]
-            x = wprime[n, rows, :] - alpha * v - times(vprev[n, rows, :], beta_prev)
+            x = wprime[n, rows, :] - times(v, alpha) - times(vprev[n, rows, :], beta_prev)
             vprev[n, rows, :] = v
             wprime[n, rows, :] = x
             vy[0, n, rows, :] = times(x, small)
@@ -468,18 +475,28 @@
 
     lax.fori_loop(0, STEPS, step, gmax)
 
-    total, _ = ar_wait(1)
-    norm_v = jnp.sqrt(vec(total))
-    inv = 1.0 / norm_v
-    norms[STEPS] = norm_v
+    store = pltpu.make_async_copy(wprime, out_w, iosem.at[0])
+    store.start()
+    ar_wait(1)
+    norms[STEPS] = jnp.sqrt(ar_read(1)[0])
+    for j in range(STEPS):
+        out_s[STEPS + j] = norms[j + 1]
+    store.wait()
+
+
+def last_kernel(ts, w, s, out_v, alpha, beta, psi_v, iosem):
+    LB = min(128, ts)
+    inv = 1.0 / s[2 * STEPS - 1][:, :LB]
+    blocks = range(2 * ts // LB)
     stores = [pltpu.make_async_copy(psi_v.at[b].reshape(ts, 2, LB), out_v.at[:, :, pl.ds(b * LB, LB)], iosem.at[b]) for b in blocks]
     for b, store in enumerate(stores):
         for sp in range(2):
-            psi_v[b, pl.ds(sp, ts, stride=2), :] = times(
-                wprime[2 * (b * LB // ts) + sp, :, pl.ds(b * LB % ts, LB)], inv)
+            x = w[2 * (b * LB // ts) + sp, :, pl.ds(b * LB % ts, LB)]
+            psi_v[b, pl.ds(sp, ts, stride=2), :] = (x.reshape(ts // 8, 8, LB) * inv[None]).reshape(ts, LB)
         store.start()
     for j in range(STEPS):
-        out_ab[STEPS + j] = jnp.max(norms[j + 1])
+        alpha[j] = jnp.max(s[j])
+        beta[j] = jnp.max(s[STEPS + j])
     for store in stores:
         store.wait()
 
@@ -491,24 +508,36 @@
     any_space = pl.BlockSpec(memory_space=pl.ANY)
     dma, V = pltpu.SemaphoreType.DMA, pltpu.VMEM
     smem = pl.BlockSpec(memory_space=pltpu.SMEM)
-    out_v, out_ab = pl.pallas_call(
+    vmem = pl.BlockSpec(memory_space=pltpu.VMEM)
+    W8 = min(128, ts)
+    out_w, out_s = pl.pallas_call(
         functools.partial(lanczos_kernel, ts, nd),
-        out_shape=(jax.ShapeDtypeStruct((ts, 2, 2 * ts), F32), jax.ShapeDtypeStruct((2 * STEPS,), F32)),
+        out_shape=(jax.ShapeDtypeStruct((4, ts, ts), F32), jax.ShapeDtypeStruct((2 * STEPS, 8, W8), F32)),
         in_specs=[any_space] * 4,
-        out_specs=(any_space, smem),
+        out_specs=(any_space, vmem),
         scratch_shapes=[
             V((2 * ts // min(128, ts), 2 * ts, min(128, ts)), F32), V((2 * nd, 2, nd), F32), V((STEPS + 1, 8, min(128, ts)), F32),
+            V((2, 8, min(128, ts)), F32),
             V((8, 4, ts, ts), F32), V((4, ts, ts), F32), V((4, ts, ts), F32), V((4, ts, ts), F32),
             V((max(20, 2 * nd), ts, ts), F32), V((2 * nd, ts, 2 * ts), F32), V((3, nd, 2 * ts, 2 * ts), BF16),
             V((3, ts, ts), BF16), V((3, ts, ts), BF16), V((3, 2, ts, ts), BF16), V((3, 2, ts, ts), BF16),
-            V((3, ts, 4 * ts), BF16), V((2 * nd * KRON, 12 * nd * KRON), BF16),
+            V((3, ts, 4 * ts), BF16), V((4 * nd * KRON, 256), BF16), V((2 * nd * KRON, 256), BF16),
             V((2, 2, 128), F32), V((2, NDEV, 2, 128), F32),
             dma((2,)), dma((2,)), dma((8,)), dma((8,)), dma((10,)), dma((10,)), dma((2,)), dma((2,)), dma((4,)), dma,
             pltpu.SemaphoreType.REGULAR, pltpu.SemaphoreType.REGULAR,
         ],
         compiler_params=pltpu.CompilerParams(vmem_limit_bytes=67043328, has_side_effects=True, collective_id=0),
     )(psi_blk, w_in, lt, rt)
-    return out_ab[:STEPS], out_ab[STEPS:], out_v
+    scalars = jax.ShapeDtypeStruct((STEPS,), F32)
+    out_v, alpha, beta = pl.pallas_call(
+        functools.partial(last_kernel, ts),
+        out_shape=(jax.ShapeDtypeStruct((ts, 2, 2 * ts), F32), scalars, scalars),
+        in_specs=[vmem, vmem],
+        out_specs=(any_space, smem, smem),
+        scratch_shapes=[V((2 * ts // W8, 2 * ts, W8), F32), dma((4,))],
+        compiler_params=pltpu.CompilerParams(vmem_limit_bytes=8 << 20),
+    )(out_w, out_s)
+    return alpha, beta, out_v
 
 
 def build(mesh, ts, nd):

time: 823 us -> 827 us (level)
  no operation moved by 1% of the time
where the time goes in v4:
time: 827 us
  Pallas kernels  825 us (100%)
    pallas_call x1, Pallas kernels, local_steps(): pl.pallas_call(functools.partial(lanczos_kernel, ts, nd), out_shape=(jax....  823 us

profile of v4, /device:TPU:0, one launch (start us, length us, event | category | flops | bytes accessed | tf_op | source)
XLA Modules:
  0.0 827.2 jit_solution(8189912469984774519)
XLA Ops:
  0.6 823.0 %shard_map.67 = (f32[4,256,256]{2,1,0:T(8,128)}, f32[8,8,128]{2,1,0:T(8,128)}) custom-call(f32[256,2,512]{2,1,0:T(2,128)} %psi.1, f32[28,2,14]{2,1,0:T(2,128)} %bitcast.9, f32[14,256,2048]{2,1,0:T(8,128)} %bitcast.8, f32[56,128,2048]{2,1,0:T(8,128)} %bitcast.7), custom_call_target="tpu_custom_call" | custom-call | tf_op jit(solution)/shard_map/pallas_call | solution.py:513
  823.6 0.0 copy-start
  823.6 1.2 copy-done
  824.9 0.0 copy-start.1
  824.9 0.8 copy-done.1
  825.6 1.5 shard_map.68
Async XLA Ops:
  823.6 1.2 copy-start
  824.9 0.8 copy-start.1

commit v5 on v4

--- a/solution.py
+++ b/solution.py
@@ -32,14 +32,14 @@
 
 
 def lanczos_kernel(ts, nd, psi, w_in, lt, rt, out_w, out_s,
-                   psi_v, wv, norms, mults, vy, vcur, vprev, wprime, recv, t1, t2, l0, l1, r0, r1, vp, wk_a, wk_b, ar_src, ar_recv,
+                   psi_v, wv, norms, mults, vy, vcur, vprev, wprime, recv, t1, t2, l0, l1, r0, r1, l2, vp, wk_a, wk_b, ar_src, ar_recv,
                    lsem, rsem, vsend, vrecv, ysend, yrecv, asend, arecv, iosem, wsem, fwd_ok, back_ok):
     row, col = lax.axis_index("row"), lax.axis_index("col")
     me = col * NROW + row
     core, xx, yy = mod(row, 2), mod(div(row, 2), 2), div(row, 4)
     hs = ts // 2
     kron = 2 * nd * KRON
-    lps, rps = (l0, l1), (r0, r1)
+    lps, rps = (l0, l1, l2), (r0, r1)
 
     def six(lhs, rhs):
         a = [x for p, n in PASSES for x in lhs[:n]]
@@ -68,10 +68,11 @@
         return pl.multiple_of(row_of(mod(g, 8)) * ts, ts)
 
     def l_batch(slot, a0, a1):
-        pltpu.make_async_copy(lt.at[pl.ds(1, nd - 1), :, pl.ds(pl.multiple_of(a0, ts), ts)],
-                              recv.at[pl.ds(nd * slot, nd - 1)], lsem.at[slot]).start()
-        pltpu.make_async_copy(lt.at[pl.ds(0, 1), :, pl.ds(pl.multiple_of(a1, ts), ts)],
-                              recv.at[pl.ds(nd * slot + nd - 1, 1)], lsem.at[slot]).start()
+        if nd > 2:
+            pltpu.make_async_copy(lt.at[pl.ds(2, nd - 2), :, pl.ds(pl.multiple_of(a0, ts), ts)],
+                                  recv.at[pl.ds(nd * slot, nd - 2)], lsem.at[slot]).start()
+        pltpu.make_async_copy(lt.at[pl.ds(0, 2), :, pl.ds(pl.multiple_of(a1, ts), ts)],
+                              recv.at[pl.ds(nd * slot + nd - 2, 2)], lsem.at[slot]).start()
 
     def l_batch_wait(slot):
         ref = recv.at[pl.ds(nd * slot, nd)]
@@ -104,7 +105,10 @@
         for b in range(ts // SB):
             rows = pl.ds(b * SB, SB)
             for p, x in enumerate(split3(recv[nd * slot + k, rows, :])):
-                dst[p, rows, :] = x
+                dst[p, pl.ds(k % 2 * ts + b * SB, SB), :] = x
+
+    def set_of(pair):
+        return 0 if pair == 0 else 2 - pair % 2
 
     def r_split(slot, k, dst):
         hh, kk = k // half, k % half
@@ -198,8 +202,8 @@
         load.start()
     w_load = pltpu.make_async_copy(w_in, wv, wsem)
     w_load.start()
-    l_first = pltpu.make_async_copy(lt.at[pl.ds(0, 1), :, pl.ds(pl.multiple_of(row * ts, ts), ts)],
-                                    recv.at[pl.ds(2 * nd - 1, 1)], lsem.at[1])
+    l_first = pltpu.make_async_copy(lt.at[pl.ds(0, 2), :, pl.ds(pl.multiple_of(row * ts, ts), ts)],
+                                    recv.at[pl.ds(2 * nd - 2, 2)], lsem.at[1])
     l_first.start()
     zero_i = jnp.int32(0)
     r_first = pltpu.make_async_copy(rt.at[pl.ds(0, 4), :, pl.ds(r_start(zero_i), ts)],
@@ -239,7 +243,8 @@
         wk_a[pl.ds(k * kron, kron), :] = wide[k].astype(BF16)
     wk_b[...] = jnp.where(lane < kron, wide[2], wide[0]).astype(BF16)
     l_first.wait()
-    l_split(1, nd - 1, l0)
+    for k in range(2):
+        l_split(1, nd - 2 + k, l0)
     r_first.wait()
     r_split(1, nd - 1, r0)
     ar_wait(0)
@@ -258,13 +263,15 @@
         low = lax.broadcasted_iota(jnp.int32, a.shape, 1) < 4
         return jnp.where(low, a, pltpu.roll(b, 4, 1)), jnp.where(low, pltpu.roll(a, 4, 1), b)
 
-    def t1_chunk(pieces, l, keep):
+    def t1_pair(pieces, pair, keep):
         got = six([pieces[k] for k in range(3)], [vp[p] for p in range(3)])
-        for bh in range(2):
-            both = swap(got[:, 2 * bh * ts:(2 * bh + 1) * ts], got[:, (2 * bh + 1) * ts:(2 * bh + 2) * ts])
-            for e in range(2):
-                at = (2 * l + e, slice(None), pl.ds(bh * ts, ts))
-                t1[at] = jnp.where(keep, t1[at], 0.0) + both[e].reshape(ts, ts)
+        for k in range(2):
+            one = got[k * ts:(k + 1) * ts]
+            for bh in range(2):
+                both = swap(one[:, 2 * bh * ts:(2 * bh + 1) * ts], one[:, (2 * bh + 1) * ts:(2 * bh + 2) * ts])
+                for e in range(2):
+                    at = (4 * pair + 2 * k + e, slice(None), pl.ds(bh * ts, ts))
+                    t1[at] = jnp.where(keep, t1[at], 0.0) + both[e].reshape(ts, ts)
 
     def t1_group(g, carry):
         slot, a1, a2 = carry
@@ -292,9 +299,10 @@
                 rows = pl.ds(b * SB, SB)
                 for p, x in enumerate(split3(vy[g, n, rows, :])):
                     vp[p, rows, pl.ds(n * ts, ts)] = x
-        for k in range(nd):
-            l_split(slot, k, lps[(k + 1) % 2])
-            t1_chunk(lps[k % 2], k, g > 0)
+        for pair in range(nd // 2):
+            for k in range(2):
+                l_split(slot, 2 * pair + k, lps[set_of((pair + 1) % (nd // 2))])
+            t1_pair(lps[set_of(pair)], pair, g > 0)
         return 1 - slot, a2, l_start(g + 3)
 
     t2_rows = min(128, hs)
@@ -351,17 +359,14 @@
             r_batch(1 - slot, d1, d2)
 
         r_batch_wait(slot)
-        total = [None, None]
+        total = None
         for k in range(nd):
             r_split(slot, k, rps[(k + 1) % 2])
             if k == 1:
                 d3 = r_start(i + 3)
-            for q in range(2):
-                got = six([t2[p, k, pl.ds(q * ts, ts)] for p in range(3)],
-                          [rps[k % 2][p].reshape(2 * ts, ts) for p in range(3)])
-                total[q] = got if total[q] is None else total[q] + got
-        for q in range(2):
-            vy[4 + dm, 2 * h + q] = total[q]
+            got = six([t2[p, k] for p in range(3)], [rps[k % 2][p].reshape(2 * ts, ts) for p in range(3)])
+            total = got if total is None else total + got
+        vy[4 + dm, pl.ds(2 * h, 2)] = total.reshape(2, ts, ts)
 
         @pl.when(i == 2 * mz)
         def _():
@@ -520,7 +525,8 @@
             V((2, 8, min(128, ts)), F32),
             V((8, 4, ts, ts), F32), V((4, ts, ts), F32), V((4, ts, ts), F32), V((4, ts, ts), F32),
             V((max(20, 2 * nd), ts, ts), F32), V((2 * nd, ts, 2 * ts), F32), V((3, nd, 2 * ts, 2 * ts), BF16),
-            V((3, ts, ts), BF16), V((3, ts, ts), BF16), V((3, 2, ts, ts), BF16), V((3, 2, ts, ts), BF16),
+            V((3, 2 * ts, ts), BF16), V((3, 2 * ts, ts), BF16), V((3, 2, ts, ts), BF16), V((3, 2, ts, ts), BF16),
+            V((3, 2 * ts, ts), BF16),
             V((3, ts, 4 * ts), BF16), V((4 * nd * KRON, 256), BF16), V((2 * nd * KRON, 256), BF16),
             V((2, 2, 128), F32), V((2, NDEV, 2, 128), F32),
             dma((2,)), dma((2,)), dma((8,)), dma((8,)), dma((10,)), dma((10,)), dma((2,)), dma((2,)), dma((4,)), dma,

time: 827 us -> 825 us (level)
  no operation moved by 1% of the time
where the time goes in v5:
time: 825 us; the launch traced here: 824 us
  Pallas kernels  822 us (100%)
    pallas_call x1, Pallas kernels, local_steps(): pl.pallas_call(functools.partial(lanczos_kernel, ts, nd), out_shape=(jax....  820 us

profile of v5, /device:TPU:0, one launch (start us, length us, event | category | flops | bytes accessed | tf_op | source)
XLA Modules:
  0.0 824.5 jit_solution(13017555067813877078)
XLA Ops:
  0.6 820.3 %shard_map.67 = (f32[4,256,256]{2,1,0:T(8,128)}, f32[8,8,128]{2,1,0:T(8,128)}) custom-call(f32[256,2,512]{2,1,0:T(2,128)} %psi.1, f32[28,2,14]{2,1,0:T(2,128)} %bitcast.9, f32[14,256,2048]{2,1,0:T(8,128)} %bitcast.8, f32[56,128,2048]{2,1,0:T(8,128)} %bitcast.7), custom_call_target="tpu_custom_call" | custom-call | tf_op jit(solution)/shard_map/pallas_call | solution.py:518
  821.0 0.0 copy-start
  821.0 1.2 copy-done
  822.2 0.0 copy-start.1
  822.2 0.8 copy-done.1
  822.9 1.5 shard_map.68
Async XLA Ops:
  821.0 1.2 copy-start
  822.2 0.8 copy-start.1
